TPU v7x, 32 devices: a whole 2x2x4 slice. The times are simulated.
32 devices in a mesh: groups: 2 (over y), seq: 4 (over z), fsdp: 2 (over x), sub: 2 (over core).
Axes of the slice: x: 2, y: 2, z: 4, core: 2. Of those that a mesh axis runs over, the one named last changes fastest.
Arguments:
- tokens: bfloat16 [2048, 8192], P(('groups', 'seq')), parts along dimension 0, may hold values from -400 to 400
- norm_gain: float32 [8192], replicated, may hold values from 0.1 to 1.9
- w_query: bfloat16 [8, 16, 8192], P(('seq', 'sub'), 'fsdp'), may hold values from -0.0625 to 0.0625
- w_key: bfloat16 [8, 16, 8192], P(('seq', 'sub'), 'fsdp'), may hold values from -0.0625 to 0.0625
- w_value: bfloat16 [8, 128, 8192], P(('seq', 'sub'), 'fsdp'), may hold values from -5 to 5
- head_gain: float32 [128], replicated, may hold values from 0.1 to 1.9
- w_out: bfloat16 [8, 128, 8192], P('seq', None, ('fsdp', 'sub')), may hold values from -0.1875 to 0.1875
Outputs:
- mixed: bfloat16 [2048, 8192], P(('groups', 'seq'), ('fsdp', 'sub')), parts along dimension 0
There are 2 independent parts, one for each index of `groups`. A program takes and returns all parts, laid end to end along the dimension named above; an argument that names none is the same for every part. Nothing has to cross between parts.
All inputs are finite; a program needn't handle non-finite values.
Results may differ from a plain program's by a relative error of at most 0.0084.
Values may be sent and summed in bfloat16 or wider, within the bound.
A program may use at most 64 MiB of HBM per device.

v0:
```python
import functools

import jax
import jax.numpy as jnp
from jax import lax
from jax.experimental import pallas as pl
from jax.experimental.pallas import tpu as pltpu
from jax.sharding import PartitionSpec as P

MESH = pl.DeviceIdType.MESH
F32 = jnp.float32
BF16 = jnp.bfloat16


def kernel(
    n,
    nf,
    ns,
    pieces,
    out_pieces,
    w_count,
    tok_hbm,
    gain_ref,
    head_gain_ref,
    wo_hbm,
    *rest,
):
    kernel_body(
        n, nf, ns, pieces, out_pieces, tok_hbm, gain_ref, head_gain_ref, wo_hbm,
        rest[:w_count], *rest[w_count:]
    )


def kernel_body(
    n,
    nf,
    ns,
    pieces,
    out_pieces,
    tok_hbm,
    gain_ref,
    head_gain_ref,
    wo_hbm,
    w_hbm,
    out_ref,
    tok_ref,
    w_ref,
    wo_ref,
    load_sem,
    normed,
    wbuf,
    wobuf,
    qk_send,
    v_send,
    qk_all,
    v_all,
    q_full,
    k_full,
    num_send,
    num_all,
    attended,
    total,
    w_zrecv,
    w_yrecv,
    w_right,
    w_left,
    w_across,
    o_zrecv,
    o_yrecv,
    o_right,
    o_left,
    o_across,
    qk_ssem,
    qk_rsem,
    v_ssem,
    v_rsem,
    num_ssem,
    num_rsem,
    sib_ssem,
    sib_rsem,
):
    group = lax.axis_index("groups")
    me = lax.axis_index("seq")
    my_f = lax.axis_index("fsdp")
    my_s = lax.axis_index("sub")
    tokens, width = tok_ref.shape

    loads = []
    row = 0
    for k, source in enumerate(w_hbm):
        size = source.shape[0]
        target = w_ref.at[pl.ds(row, size)] if len(w_hbm) > 1 else w_ref
        loads.append(pltpu.make_async_copy(source, target, load_sem.at[k]))
        row += size
    tok_load = pltpu.make_async_copy(tok_hbm, tok_ref, load_sem.at[len(w_hbm)])
    wo_load = pltpu.make_async_copy(wo_hbm, wo_ref, load_sem.at[len(w_hbm) + 1])
    for load in loads + [tok_load, wo_load]:
        load.start()

    peers = [
        {"seq": lax.rem(me + dz, n), "fsdp": lax.rem(my_f + df, nf)}
        for dz in range(n)
        for df in range(nf)
        if dz or df
    ]
    peers += [
        {"fsdp": lax.rem(my_f + df, nf), "sub": lax.rem(my_s + ds, ns)}
        for df in range(nf)
        for ds in range(1, ns)
    ]
    peers += [{"groups": 1 - group}]
    barrier = pltpu.get_barrier_semaphore()
    for peer in peers:
        pl.semaphore_signal(barrier, inc=1, device_id=peer, device_id_type=MESH)
    pl.semaphore_wait(barrier, len(peers))
    for load in loads:
        load.wait()
    span = width // (2 * pieces)
    qk_rows = qk_all.shape[2]
    half_rows = qk_rows // 2

    def own_w(c):
        start = pl.multiple_of((group * pieces + c) * span, span)
        return w_ref.at[:, pl.ds(start, span)]

    def own_o(c):
        return wo_ref.at[group, c]

    class Stream:
        def __init__(self, own, buf, count, zrecv, yrecv, right, left, across):
            self.own, self.buf, self.count = own, buf, count
            self.zrecv, self.yrecv = zrecv, yrecv
            self.right_sem, self.left_sem, self.across_sem = right, left, across

        def along(self, o, c, sems, target, own):
            slot = self.buf.at[o, group, c]
            return pltpu.make_async_remote_copy(
                src_ref=self.own(c) if own else slot,
                dst_ref=slot,
                send_sem=sems.at[o, c],
                recv_sem=self.zrecv.at[o, c],
                device_id={"seq": target},
                device_id_type=MESH,
            )

        def right(self, o, c, own=False):
            return self.along(o, c, self.right_sem, me + 1, own)

        def left(self, o, c, own=False):
            return self.along(o, c, self.left_sem, me - 1, own)

        def across(self, o, c, half):
            slot = self.buf.at[o, half, c]
            return pltpu.make_async_remote_copy(
                src_ref=slot,
                dst_ref=slot,
                send_sem=self.across_sem.at[o, c],
                recv_sem=self.yrecv.at[o, c],
                device_id={"groups": 1 - group},
                device_id_type=MESH,
            )

        def begin(self):
            for c in range(self.count):

                @pl.when(me + 1 < n)
                def _():
                    self.right(me, c, True).start()

                @pl.when(me >= 1)
                def _():
                    self.left(me, c, True).start()

        def relay(self, r, between=None):
            for c in range(self.count):
                if between is not None and c == self.count // 2:
                    between()

                @pl.when(me >= r)
                def _():
                    o = me - r
                    self.right(o, c).wait_recv()

                    @pl.when(me + 1 < n)
                    def _():
                        self.right(o, c).start()

                    self.across(o, c, group).start()

                @pl.when(me + r < n)
                def _():
                    o = me + r
                    self.left(o, c).wait_recv()

                    @pl.when(me >= 1)
                    def _():
                        self.left(o, c).start()

                    self.across(o, c, group).start()

        def arrive(self, o):
            for c in range(self.count):
                self.across(o, c, 1 - group).wait_recv()

        def finish(self):
            for r in range(n):
                for c in range(self.count):

                    @pl.when((me >= r) & (me + 1 < n))
                    def _():
                        self.right(me - r, c, r == 0).wait_send()

                    @pl.when((me + r < n) & (me >= 1))
                    def _():
                        self.left(me + r, c, r == 0).wait_send()

                    if r > 0:

                        @pl.when(me >= r)
                        def _():
                            self.across(me - r, c, group).wait_send()

                        @pl.when(me + r < n)
                        def _():
                            self.across(me + r, c, group).wait_send()

    w_stream = Stream(own_w, wbuf, pieces, w_zrecv, w_yrecv, w_right, w_left, w_across)
    o_stream = Stream(own_o, wobuf, out_pieces, o_zrecv, o_yrecv, o_right, o_left, o_across)

    w_stream.begin()
    wo_load.wait()
    at_end = (me == 0) | (me == n - 1)

    @pl.when(at_end)
    def _():
        o_stream.begin()

    tok_load.wait()

    row_step = 16

    def norm_rows(i, carry):
        rows = pl.ds(pl.multiple_of(i * row_step, row_step), row_step)
        sumsq = jnp.zeros((row_step, 1), F32)
        for c in range(2 * pieces):
            part = tok_ref[rows, c * span : (c + 1) * span].astype(F32)
            sumsq = sumsq + jnp.sum(part * part, axis=1, keepdims=True)
        scale = lax.rsqrt(sumsq / width + 1e-05)
        for c in range(2 * pieces):
            cols = slice(c * span, (c + 1) * span)
            part = tok_ref[rows, cols].astype(F32)
            normed[c, rows, :] = (part * scale * gain_ref[:, cols]).astype(BF16)
        return carry

    lax.fori_loop(0, tokens // row_step, norm_rows, 0)

    def contract(weights, acts):
        return lax.dot_general(weights, acts, (((1,), (1,)), ((), ())), preferred_element_type=F32)

    def qk_copy(o, source, other_f, token_block, f_from):
        return pltpu.make_async_remote_copy(
            src_ref=source,
            dst_ref=qk_all.at[token_block, f_from],
            send_sem=qk_ssem.at[o, other_f],
            recv_sem=qk_rsem.at[token_block, f_from],
            device_id={"seq": o, "fsdp": other_f},
            device_id_type=MESH,
        )

    def v_copy(o, token_block):
        return pltpu.make_async_remote_copy(
            src_ref=v_send.at[o],
            dst_ref=v_all.at[token_block],
            send_sem=v_ssem.at[o],
            recv_sem=v_rsem.at[token_block],
            device_id={"seq": o},
            device_id_type=MESH,
        )

    def project_own():
        acc = jnp.zeros((w_ref.shape[0], tokens), F32)
        for c in range(2 * pieces):
            acc = acc + contract(w_ref[:, c * span : (c + 1) * span], normed[c])
        qk_all[me, my_f] = acc[:qk_rows].astype(BF16)
        v_all[me] = acc[qk_rows:].astype(BF16)
        for df in range(1, nf):
            other = lax.rem(my_f + df, nf)
            qk_copy(me, qk_all.at[me, my_f], other, me, my_f).start()

    def project(o):
        def body(c, acc):
            return acc + contract(wbuf[o, c // pieces, c % pieces], normed[c])

        acc = lax.fori_loop(0, 2 * pieces, body, jnp.zeros((w_ref.shape[0], tokens), F32))
        qk_send[o] = acc[:qk_rows].astype(BF16)
        v_send[o] = acc[qk_rows:].astype(BF16)
        for df in range(nf):
            qk_copy(o, qk_send.at[o], lax.rem(my_f + df, nf), me, my_f).start()
        v_copy(o, me).start()

    def both(r, action):
        @pl.when(me >= r)
        def _():
            action(me - r)

        @pl.when(me + r < n)
        def _():
            action(me + r)

    def take(o):
        w_stream.arrive(o)
        project(o)

    project_own()
    for r in range(1, n):
        if r == n - 1:

            @pl.when(jnp.logical_not(at_end))
            def _():
                o_stream.begin()

        w_stream.relay(r, functools.partial(both, r - 1, take) if r > 1 else None)

    o_stream.relay(1, functools.partial(both, n - 1, take))

    def gather_heads():
        for d in range(1, n):
            t = lax.rem(me + d, n)
            v_copy(me, t).wait_recv()
            for df in range(nf):
                qk_copy(me, qk_all.at[t, df], 0, t, df).wait_recv()
        for df in range(1, nf):
            other = lax.rem(my_f + df, nf)
            qk_copy(me, qk_all.at[me, other], other, me, other).wait_recv()

        for t in range(n):
            parts = [qk_all[t, f].astype(F32) for f in range(nf)]
            q_full[t] = jnp.concatenate([p[:half_rows] for p in parts], 0).astype(BF16)
            k_full[t] = jnp.concatenate([p[half_rows:] for p in parts], 0).astype(BF16)

    channels = v_all.shape[1]
    key_pos = lax.broadcasted_iota(jnp.int32, (tokens, tokens), 0)
    query_pos = lax.broadcasted_iota(jnp.int32, (tokens, tokens), 1)

    def numerator(t):
        queries = q_full[t]

        def body(j, acc):
            scores = lax.dot_general(
                k_full[j], queries, (((0,), (0,)), ((), ())), preferred_element_type=F32
            )
            value = 1.0 + scores * 0.25 + scores * scores * 0.03125
            weight = jnp.where(key_pos + (j - t) * tokens <= query_pos, value, 0.0).astype(BF16)
            return acc + jnp.dot(v_all[j], weight, preferred_element_type=F32)

        acc = lax.fori_loop(0, t + 1, body, jnp.zeros((channels, tokens), F32))
        return acc.astype(BF16)

    def num_copy(t, head_block):
        return pltpu.make_async_remote_copy(
            src_ref=num_send.at[t],
            dst_ref=num_all.at[head_block, my_f, my_s],
            send_sem=num_ssem.at[t],
            recv_sem=num_rsem.at[head_block],
            device_id={"seq": t},
            device_id_type=MESH,
        )

    def sib_copy(o, to_f, to_s, from_f, from_s):
        slot = num_all.at[o, from_f, from_s]
        return pltpu.make_async_remote_copy(
            src_ref=slot,
            dst_ref=slot,
            send_sem=sib_ssem.at[o, to_f, to_s],
            recv_sem=sib_rsem.at[o, from_f, from_s],
            device_id={"fsdp": to_f, "sub": to_s},
            device_id_type=MESH,
        )

    def siblings():
        for df in range(nf):
            for ds in range(ns):
                if df or ds:
                    yield lax.rem(my_f + df, nf), lax.rem(my_s + ds, ns)

    def attend():
        gather_heads()
        for d in range(1, n):
            t = lax.rem(me + d, n)
            num_send[t] = numerator(t)
            num_copy(t, me).start()
        num_all[me, my_f, my_s] = numerator(me)
        for f, s in siblings():
            sib_copy(me, f, s, my_f, my_s).start()

    def spread():
        for d in range(1, n):
            o = lax.rem(me + d, n)
            num_copy(o, o).wait_recv()
            for f, s in siblings():
                sib_copy(o, f, s, my_f, my_s).start()

    for r in range(2, n):
        o_stream.relay(r, {2: attend, 3: spread}.get(r))

    for d in range(n):
        o = lax.rem(me + d, n)
        for f, s in siblings():
            sib_copy(o, f, s, f, s).wait_recv()

    head_width = nf * channels

    def attend_block(o, carry):
        for s in range(ns):
            whole = jnp.concatenate([num_all[o, f, s] for f in range(nf)], 0).astype(F32)
            meansq = jnp.sum(whole * whole, axis=0, keepdims=True) / head_width
            scaled = (whole * lax.rsqrt(meansq + 1e-06)).T * head_gain_ref[...]
            attended[o, :, s * head_width : (s + 1) * head_width] = scaled.astype(BF16)
        return carry

    lax.fori_loop(0, n, attend_block, 0)

    columns = out_ref.shape[1]
    depth = ns * head_width

    total[...] = jnp.dot(
        attended[me], wo_ref[...].reshape(depth, columns), preferred_element_type=F32
    )

    def multiply(o):
        o_stream.arrive(o)
        total[...] += jnp.dot(
            attended[o], wobuf[o].reshape(depth, columns), preferred_element_type=F32
        )

    for r in range(1, n):
        both(r, multiply)
    out_ref[...] = total[...].astype(BF16)

    w_stream.finish()
    o_stream.finish()
    for d in range(n):
        o = lax.rem(me + d, n)
        for df in range(nf):
            if d or df:
                other = lax.rem(my_f + df, nf)
                source = qk_send.at[o] if d else qk_all.at[me, my_f]
                qk_copy(o, source, other, me, my_f).wait_send()
        if d:
            v_copy(o, me).wait_send()
            num_copy(o, me).wait_send()
        for f, s in siblings():
            sib_copy(o, f, s, my_f, my_s).wait_send()


def per_device(sizes, tokens, norm_gain, w_query, w_key, w_value, head_gain, w_out):
    n, nf, ns = sizes
    shards = [w_query[0], w_key[0], w_value[0]]
    if any(shard.shape[0] % 8 for shard in shards):
        shards = [jnp.concatenate(shards, 0)]
    rows, width = sum(shard.shape[0] for shard in shards), tokens.shape[1]
    count = tokens.shape[0]
    qk_rows = w_query.shape[1] + w_key.shape[1]
    channels = w_value.shape[1]
    head_width, columns = w_out.shape[1], w_out.shape[2]
    pieces = max(1, 16 // n)
    out_pieces = max(1, 16 // n)
    wo = w_out.reshape(ns, out_pieces, head_width // out_pieces, columns)
    hbm = pl.BlockSpec(memory_space=pl.ANY)
    vmem = pl.BlockSpec(memory_space=pltpu.VMEM)
    dma = pltpu.SemaphoreType.DMA
    return pl.pallas_call(
        functools.partial(kernel, n, nf, ns, pieces, out_pieces, len(shards)),
        out_shape=jax.ShapeDtypeStruct((count, columns), BF16),
        in_specs=[hbm, vmem, vmem, hbm] + [hbm] * len(shards),
        out_specs=vmem,
        scratch_shapes=[
            pltpu.VMEM(tokens.shape, BF16),
            pltpu.VMEM((rows, width), BF16),
            pltpu.VMEM(wo.shape, BF16),
            dma((len(shards) + 2,)),
            pltpu.VMEM((2 * pieces, count, width // (2 * pieces)), BF16),
            pltpu.VMEM((n, 2, pieces, rows, width // (2 * pieces)), BF16),
            pltpu.VMEM((n,) + wo.shape, BF16),
            pltpu.VMEM((n, qk_rows, count), BF16),
            pltpu.VMEM((n, channels, count), BF16),
            pltpu.VMEM((n, nf, qk_rows, count), BF16),
            pltpu.VMEM((n, channels, count), BF16),
            pltpu.VMEM((n, nf * qk_rows // 2, count), BF16),
            pltpu.VMEM((n, nf * qk_rows // 2, count), BF16),
            pltpu.VMEM((n, channels, count), BF16),
            pltpu.VMEM((n, nf, ns, channels, count), BF16),
            pltpu.VMEM((n, count, ns * head_width), BF16),
            pltpu.VMEM((count, columns), F32),
        ]
        + [dma((n, pieces))] * 5
        + [dma((n, out_pieces))] * 5
        + [
            dma((n, nf)),
            dma((n, nf)),
            dma((n,)),
            dma((n,)),
            dma((n,)),
            dma((n,)),
            dma((n, nf, ns)),
            dma((n, nf, ns)),
        ],
        compiler_params=pltpu.CompilerParams(
            collective_id=0, has_side_effects=True, vmem_limit_bytes=60 * 1024 * 1024
        ),
    )(tokens, norm_gain.reshape(1, -1), head_gain.reshape(1, -1), wo, *shards)


def solution(mesh):
    in_specs = (
        P(("groups", "seq"), None),
        P(),
        P(("seq", "sub"), "fsdp", None),
        P(("seq", "sub"), "fsdp", None),
        P(("seq", "sub"), "fsdp", None),
        P(),
        P("seq", None, ("fsdp", "sub")),
    )
    out_specs = P(("groups", "seq"), ("fsdp", "sub"))
    sizes = (mesh.shape["seq"], mesh.shape["fsdp"], mesh.shape["sub"])
    return jax.shard_map(
        functools.partial(per_device, sizes),
        mesh=mesh,
        in_specs=in_specs,
        out_specs=out_specs,
        check_vma=False,
    )
```

profile of v0, /device:TPU:0, one launch (start us, length us, event | category | flops | bytes accessed | tf_op | source)
XLA Modules:
  0.0 99.8 jit_solution(701053971173290675)
XLA Ops:
  0.0 97.5 %shard_map.73 = bf16[256,2048]{1,0:T(8,128)(2,1)} custom-call(bf16[256,8192]{1,0:T(8,128)(2,1)} %tok_hbm.1, f32[1,8192]{1,0:T(1,128)} %bitcast.10, f32[1,128]{1,0:T(1,128)} %bitcast.11, bf16[2,4,32,2048]{3,2,1,0:T(8,128)(2,1)} %bitcast.6, bf16[8,8192]{1,0:T(8,128)(2,1)} %bitcast.8, bf16[8,8192]{1,0:T(8,128)(2,1)} %bitcast.9, bf16[64,8192]{1,0:T(8,128)(2,1)} %bitcast.7), custom_call_target="tpu_custom_call" | custom-call | tf_op jit(solution)/shard_map/pallas_call | solution.py:472
  97.5 2.3 %copy.9 = bf16[256,2048]{1,0:T(8,128)(2,1)} copy(bf16[256,2048]{1,0:T(8,128)(2,1)} %shard_map.73) | data formatting | bytes 2097152
where the time goes:
time: 100 us; the launch traced here: 99.8 us
  Pallas kernels  97.5 us (98%)
  local copies, waits for them, and re-layouts  2.3 us (2%)
    pallas_call x1, Pallas kernels, per_device(): pl.pallas_call(functools.partial(kernel, n, nf, ns, pieces, out_pieces, l...  97.5 us
    unnamed x1, local copies, waits for them, and re-layouts  2.3 us

commit v1 on v0

--- a/solution.py
+++ b/solution.py
@@ -451,6 +451,591 @@
             num_copy(o, me).wait_send()
         for f, s in siblings():
             sib_copy(o, f, s, my_f, my_s).wait_send()
+
+def line_kernel(
+    n,
+    pieces,
+    early,
+    row_chunks,
+    tok_hbm,
+    gain_ref,
+    head_gain_ref,
+    wo_hbm,
+    wq_hbm,
+    wk_hbm,
+    wv_hbm,
+    out_ref,
+    tok_ref,
+    wo_ref,
+    load_sem,
+    ysend,
+    xn,
+    xq,
+    wall,
+    wobuf,
+    acc,
+    part_send,
+    part_recv,
+    qk,
+    q_full,
+    kv,
+    kv_prev,
+    nacc,
+    num_send,
+    num_all,
+    attended,
+    total,
+    w_ss,
+    w_rs,
+    tok_s,
+    tok_r,
+    o_out,
+    o_in,
+    o_rs,
+    o_ac,
+    o_yr,
+    part_s,
+    part_r,
+    qk_s,
+    qk_r,
+    kv_s,
+    kv_r,
+    num_s,
+    ng_s,
+    ng_r,
+):
+    g = lax.axis_index("groups")
+    z = lax.axis_index("seq")
+    f = lax.axis_index("fsdp")
+    s = lax.axis_index("sub")
+    upper = z // (n // 2)
+    sign = 2 * upper - 1
+    out_z = z + sign
+    in_z = z - sign
+    inner = (z > 0) & (z < n - 1)
+    outer = jnp.logical_not(inner)
+    low = upper == 0
+    high = upper == 1
+    near = upper
+    second = 1 - upper
+    ends = n - 2
+    my = jnp.where(inner, upper, ends + upper)
+    sl_out = ends + upper
+    sl_far = ends + 1 - upper
+    p_own = 1 - upper
+    p_end = upper
+    tokens, width = tok_ref.shape
+    rows, span = wall.shape[2], wall.shape[3]
+    qk_rows = qk.shape[3]
+    half_rows = qk_rows // 2
+    quarter = f * 2 + s
+    q_sib = f * 2 + 1 - s
+    q_x = (1 - f) * 2 + s
+    q_diag = (1 - f) * 2 + 1 - s
+
+    loads = []
+    for c in range(pieces):
+        row = 0
+        for source in (wq_hbm, wk_hbm, wv_hbm):
+            size = source.shape[0]
+            col = pl.multiple_of((g * pieces + c) * span, span)
+            loads.append(
+                pltpu.make_async_copy(
+                    source.at[:, pl.ds(col, span)],
+                    wall.at[c, my, pl.ds(row, size)],
+                    load_sem.at[len(loads)],
+                )
+            )
+            row += size
+    wo_load = pltpu.make_async_copy(wo_hbm, wo_ref, load_sem.at[len(loads)])
+    tok_load = pltpu.make_async_copy(tok_hbm, tok_ref, load_sem.at[len(loads) + 1])
+    for load in loads + [wo_load, tok_load]:
+        load.start()
+
+    barrier = pltpu.get_barrier_semaphore()
+    for peer in ({"seq": in_z}, {"groups": 1 - g}, {"fsdp": 1 - f}, {"sub": 1 - s}):
+        pl.semaphore_signal(barrier, inc=1, device_id=peer, device_id_type=MESH)
+
+    @pl.when(inner)
+    def _():
+        pl.semaphore_signal(barrier, inc=1, device_id={"seq": out_z}, device_id_type=MESH)
+        pl.semaphore_wait(barrier, 5)
+
+    @pl.when(outer)
+    def _():
+        pl.semaphore_wait(barrier, 4)
+
+    logs = {"inner": [], "outer": [], "all": [], "low": []}
+
+    def launch(role, make, *args):
+        make(*args).start()
+        logs[role].append((make, args))
+
+    def remote(src, dst, send, recv, to):
+        return pltpu.make_async_remote_copy(
+            src_ref=src,
+            dst_ref=dst,
+            send_sem=send,
+            recv_sem=recv,
+            device_id=to,
+            device_id_type=MESH,
+        )
+
+    def w_copy(h, c):
+        slot = wall.at[c, h]
+        return remote(slot, slot, w_ss.at[h, c], w_rs.at[h, c], {"seq": in_z})
+
+    def o_copy(h, c, own, inward):
+        slot = wobuf.at[h, g, c]
+        return remote(
+            wo_ref.at[g, c] if own else slot,
+            slot,
+            (o_in if inward else o_out).at[h, c],
+            o_rs.at[h, c],
+            {"seq": in_z if inward else out_z},
+        )
+
+    def across(h, c):
+        slot = wobuf.at[h, g, c]
+        return remote(slot, slot, o_ac.at[h, c], o_yr.at[h, c], {"groups": 1 - g})
+
+    def crossed(h, c):
+        slot = wobuf.at[h, 1 - g, c]
+        remote(slot, slot, o_ac.at[h, c], o_yr.at[h, c], {"groups": 1 - g}).wait_recv()
+
+    step = tokens // row_chunks
+
+    def part_rows(r):
+        return pl.ds(r * step, step)
+
+    def y_tok(r):
+        return remote(
+            ysend.at[part_rows(r)],
+            xq.at[0, quarter, part_rows(r)],
+            tok_s.at[0, 0, r],
+            tok_r.at[0, quarter, r],
+            {"groups": 1 - g},
+        )
+
+    def z_tok(k, r):
+        src = xn.at[quarter, part_rows(r)] if k == 1 else xq.at[0, quarter, part_rows(r)]
+        return remote(
+            src,
+            xq.at[k, quarter, part_rows(r)],
+            tok_s.at[k, 0, r],
+            tok_r.at[k, quarter, r],
+            {"seq": in_z},
+        )
+
+    def spread_tok(k, c, r, kind):
+        slot = xq.at[k, c, part_rows(r)]
+        to = {"fsdp": 1 - f} if kind == 2 else {"sub": 1 - s}
+        return remote(slot, slot, tok_s.at[k, kind, r], tok_r.at[k, c, r], to)
+
+    def tok_arrive(k, c, r):
+        slot = xq.at[k, c, part_rows(r)]
+        remote(slot, slot, tok_s.at[k, 1, r], tok_r.at[k, c, r], {"sub": 1 - s}).wait_recv()
+
+    def gather_own(k, r):
+        tok_arrive(k, quarter, r)
+        launch("inner", spread_tok, k, quarter, r, 2)
+        launch("inner", spread_tok, k, quarter, r, 1)
+
+    def gather_fwd(k, r):
+        tok_arrive(k, q_x, r)
+        launch("inner", spread_tok, k, q_x, r, 3)
+
+    def gathered(k, which):
+        for r in range(row_chunks):
+            for c in which:
+                tok_arrive(k, c, r)
+
+    def part_copy(p, h):
+        return remote(
+            part_send.at[p, h],
+            part_recv.at[p, h],
+            part_s.at[p, h],
+            part_r.at[p, h],
+            {"groups": 1 - g},
+        )
+
+    def qk_copy(p, h):
+        slot = qk.at[p, h, f]
+        return remote(slot, slot, qk_s.at[p, h], qk_r.at[p, h], {"fsdp": 1 - f})
+
+    def qk_arrive(p, h):
+        slot = qk.at[p, h, 1 - f]
+        remote(slot, slot, qk_s.at[p, h], qk_r.at[p, h], {"fsdp": 1 - f}).wait_recv()
+
+    def kv_copy(p, h):
+        return remote(
+            kv.at[p, h], kv_prev.at[p, h], kv_s.at[p, h], kv_r.at[p, h], {"seq": in_z}
+        )
+
+    def num_copy(h):
+        return remote(
+            num_send.at[h], num_all.at[h, f, s], num_s.at[h], ng_r.at[h, f, s], {"seq": out_z}
+        )
+
+    def spread_num(h, ff, ss, kind):
+        slot = num_all.at[h, ff, ss]
+        to = {"fsdp": 1 - f} if kind == 1 else {"sub": 1 - s}
+        return remote(slot, slot, ng_s.at[h, kind], ng_r.at[h, ff, ss], to)
+
+    def num_arrive(h, ff, ss):
+        slot = num_all.at[h, ff, ss]
+        remote(slot, slot, ng_s.at[h, 0], ng_r.at[h, ff, ss], {"sub": 1 - s}).wait_recv()
+
+    @pl.when(inner)
+    def _():
+        for c in range(pieces):
+            for load in loads[3 * c : 3 * c + 3]:
+                load.wait()
+            launch("inner", w_copy, my, c)
+        wo_load.wait()
+        for c in range(pieces):
+            launch("inner", o_copy, my, c, True, False)
+
+    @pl.when(outer)
+    def _():
+        for load in loads:
+            load.wait()
+        wo_load.wait()
+        for c in range(early):
+            launch("outer", o_copy, my, c, True, True)
+
+    tok_load.wait()
+    row_step = 16
+
+    def norm_rows(i, carry):
+        block = pl.ds(pl.multiple_of(i * row_step, row_step), row_step)
+        sumsq = jnp.zeros((row_step, 1), F32)
+        for c in range(2 * pieces):
+            part = tok_ref[block, c * span : (c + 1) * span].astype(F32)
+            sumsq = sumsq + jnp.sum(part * part, axis=1, keepdims=True)
+        scale = lax.rsqrt(sumsq / width + 1e-05)
+
+        def column(c):
+            cols = pl.ds(pl.multiple_of(c * span, span), span)
+            part = tok_ref[block, cols].astype(F32)
+            return (part * scale * gain_ref[:, cols]).astype(BF16)
+
+        ysend[block, :] = column((1 - g) * pieces + quarter)
+        for c in range(pieces):
+            xn[c, block, :] = column(g * pieces + c)
+        return carry
+
+    per_chunk = step // row_step
+    for r in range(row_chunks):
+        lax.fori_loop(r * per_chunk, (r + 1) * per_chunk, norm_rows, 0)
+        launch("all", y_tok, r)
+
+        @pl.when(outer)
+        def _():
+            launch("outer", z_tok, 1, r)
+
+    def contract(weights, acts):
+        return lax.dot_general(weights, acts, (((1,), (1,)), ((), ())), preferred_element_type=F32)
+
+    def project(k, stack, lo, hi, fresh):
+        if fresh:
+            acc[k, stack] = jnp.zeros(acc.shape[2:], F32)
+
+        def body(c, carry):
+            weights = wall[c, 2 * stack : 2 * stack + 2].reshape(2 * rows, span)
+            acts = xn[c] if k == 3 else xq[k, c]
+            acc[k, stack] += contract(weights, acts)
+            return carry
+
+        lax.fori_loop(lo, hi, body, 0)
+
+    def send_part(k, stack):
+        p = p_own if k == 0 else p_end
+        for i in range(2):
+            h = 2 * stack + i
+            part_send[p, h] = acc[k, stack, i * rows : (i + 1) * rows].astype(BF16)
+            launch("inner", part_copy, p, h)
+
+    def finish_proj(h, own):
+        p, k = (p_own, 3) if own else (p_end, 1)
+        part_copy(p, h).wait_recv()
+        i = h % 2
+        whole = acc[k, h // 2, i * rows : (i + 1) * rows] + part_recv[p, h].astype(F32)
+        qk[p, h, f] = whole[:qk_rows].astype(BF16)
+        kv[p, h, qk_rows:] = whole[qk_rows:].astype(BF16)
+        launch("inner", qk_copy, p, h)
+
+    def finish_qk(h, own):
+        p = p_own if own else p_end
+        qk_arrive(p, h)
+        halves = [qk[p, h, i].astype(F32) for i in range(2)]
+        q_full[p, h] = jnp.concatenate([x[:half_rows] for x in halves], 0).astype(BF16)
+        kv[p, h, :qk_rows] = jnp.concatenate([x[half_rows:] for x in halves], 0).astype(BF16)
+
+        @pl.when(low)
+        def _():
+            launch("low", kv_copy, p, h)
+
+    key_pos = lax.broadcasted_iota(jnp.int32, (tokens, tokens), 0)
+    query_pos = lax.broadcasted_iota(jnp.int32, (tokens, tokens), 1)
+
+    def attend_to(source, queries, diagonal):
+        scores = lax.dot_general(
+            source[:qk_rows], queries, (((0,), (0,)), ((), ())), preferred_element_type=F32
+        )
+        value = 1.0 + scores * 0.25 + scores * scores * 0.03125
+        if diagonal:
+            value = jnp.where(key_pos <= query_pos, value, 0.0)
+        return jnp.dot(source[qk_rows:], value.astype(BF16), preferred_element_type=F32)
+
+    def prior_arrive(h):
+        for p in range(2):
+            kv_copy(p, h).wait_recv()
+
+    def numerator(h, own):
+        p = p_own if own else p_end
+        queries = q_full[p, h]
+        nacc[...] = attend_to(kv[p, h], queries, True)
+
+        @pl.when(low if own else high)
+        def _():
+            nacc[...] += attend_to(kv[1 - p, h], queries, False)
+
+        @pl.when(high)
+        def _():
+            nacc[...] += attend_to(kv_prev[0, h], queries, False) + attend_to(
+                kv_prev[1, h], queries, False
+            )
+
+        if own:
+            num_all[h, f, s] = nacc[...].astype(BF16)
+            launch("inner", spread_num, h, f, s, 1)
+            launch("inner", spread_num, h, f, s, 0)
+        else:
+            num_send[h] = nacc[...].astype(BF16)
+            launch("inner", num_copy, h)
+
+    def o_relay(role, h, c, inward):
+        o_copy(h, c, False, True).wait_recv()
+        if inward is not None:
+            launch(role, o_copy, h, c, False, inward)
+        launch(role, across, h, c)
+
+    def w_relay(c):
+        w_copy(sl_out, c).wait_recv()
+        launch("inner", w_copy, sl_out, c)
+
+    late = range(early, pieces)
+
+    @pl.when(inner)
+    def _():
+        for c in range(pieces):
+            launch("inner", o_copy, my, c, True, True)
+        for c in range(early):
+            o_relay("inner", sl_out, c, True)
+        gather_own(0, 0)
+        gather_own(1, 0)
+        gather_own(0, 1)
+        for c in range(pieces):
+            w_copy(second, c).wait_recv()
+        project(3, 0, 0, pieces, True)
+        gather_fwd(0, 0)
+        gather_own(1, 1)
+        for c in range(2):
+            o_relay("inner", second, c, False)
+        gather_fwd(1, 0)
+        gather_own(2, 0)
+        for c in range(2, pieces):
+            o_relay("inner", second, c, False)
+        gather_fwd(0, 1)
+        gathered(0, (q_sib, q_diag))
+        project(0, 0, 0, pieces, True)
+        send_part(0, 0)
+        gather_own(2, 1)
+        for c in range(early):
+            o_relay("inner", sl_far, c, False)
+        w_relay(0)
+        gather_fwd(1, 1)
+        gathered(1, (q_sib, q_diag))
+        project(1, 0, 0, pieces, True)
+        w_relay(1)
+        for h in range(2):
+            finish_proj(h, True)
+        gather_fwd(2, 0)
+        w_relay(2)
+        w_relay(3)
+        for h in range(2):
+            finish_qk(h, True)
+        gather_fwd(2, 1)
+        gathered(2, (q_sib, q_diag))
+        project(2, 0, 0, pieces, True)
+        send_part(2, 0)
+        for c in range(pieces - 1):
+            w_copy(sl_far, c).wait_recv()
+        for k in range(4):
+            project(k, 1, 0, pieces - 1, True)
+        for c in late:
+            o_relay("inner", sl_out, c, True)
+        for h in range(2):
+            finish_proj(h, False)
+        w_copy(sl_far, pieces - 1).wait_recv()
+        for k in (2, 0):
+            project(k, 1, pieces - 1, pieces, False)
+            send_part(k, 1)
+        for k in (3, 1):
+            project(k, 1, pieces - 1, pieces, False)
+        for h in range(2):
+            finish_qk(h, False)
+
+        def attention(h):
+            @pl.when(high)
+            def _():
+                prior_arrive(h)
+
+            numerator(h, False)
+            numerator(h, True)
+
+        for h in range(2):
+            attention(h)
+        for c in late:
+            o_relay("inner", sl_far, c, False)
+        for h in range(2, 4):
+            finish_proj(h, False)
+            finish_proj(h, True)
+        for h in range(2, 4):
+            finish_qk(h, False)
+            finish_qk(h, True)
+        for h in range(2, 4):
+            attention(h)
+
+    @pl.when(outer)
+    def _():
+        for r in range(row_chunks):
+            tok_arrive(0, quarter, r)
+            launch("outer", z_tok, 2, r)
+        for c in range(pieces):
+            launch("outer", w_copy, my, c)
+        for c in late:
+            launch("outer", o_copy, my, c, True, True)
+        for h in (near, second):
+            for c in range(pieces):
+                o_relay("outer", h, c, None)
+        for c in range(pieces):
+            o_relay("outer", sl_far, c, None)
+        for h in range(n):
+            num_arrive(h, f, s)
+            launch("outer", spread_num, h, f, s, 1)
+            launch("outer", spread_num, h, f, s, 0)
+
+    head_width = 2 * num_all.shape[3]
+    columns = out_ref.shape[1]
+    depth = 2 * head_width
+
+    def attend_block(h):
+        num_arrive(h, 1 - f, s)
+        launch("all", spread_num, h, 1 - f, s, 2)
+        num_arrive(h, f, 1 - s)
+        num_arrive(h, 1 - f, 1 - s)
+        for i in range(2):
+            whole = jnp.concatenate([num_all[h, j, i] for j in range(2)], 0).astype(F32)
+            meansq = jnp.sum(whole * whole, axis=0, keepdims=True) / head_width
+            scaled = (whole * lax.rsqrt(meansq + 1e-06)).T * head_gain_ref[...]
+            attended[h, :, i * head_width : (i + 1) * head_width] = scaled.astype(BF16)
+
+    def multiply(h):
+        @pl.when(my == h)
+        def _():
+            total[...] += jnp.dot(
+                attended[h], wo_ref[...].reshape(depth, columns), preferred_element_type=F32
+            )
+
+        @pl.when(my != h)
+        def _():
+            for c in range(pieces):
+                crossed(h, c)
+            total[...] += jnp.dot(
+                attended[h], wobuf[h].reshape(depth, columns), preferred_element_type=F32
+            )
+
+    total[...] = jnp.zeros(total.shape, F32)
+    for h in range(n):
+        attend_block(h)
+        multiply(h)
+    out_ref[...] = total[...].astype(BF16)
+
+    for role, gate in (("inner", inner), ("outer", outer), ("low", inner & low)):
+
+        @pl.when(gate)
+        def _():
+            for make, args in logs[role]:
+                make(*args).wait_send()
+
+    for make, args in logs["all"]:
+        make(*args).wait_send()
+
+
+def per_device_line(n, tokens, norm_gain, w_query, w_key, w_value, head_gain, w_out):
+    count, width = tokens.shape
+    shards = [w_query[0], w_key[0], w_value[0]]
+    rows = sum(shard.shape[0] for shard in shards)
+    qk_rows = w_query.shape[1] + w_key.shape[1]
+    channels = w_value.shape[1]
+    head_width, columns = w_out.shape[1], w_out.shape[2]
+    pieces, early, row_chunks = 4, 2, 2
+    span = width // (2 * pieces)
+    wo = w_out.reshape(2, pieces, head_width // pieces, columns)
+    hbm = pl.BlockSpec(memory_space=pl.ANY)
+    vmem = pl.BlockSpec(memory_space=pltpu.VMEM)
+    dma = pltpu.SemaphoreType.DMA
+    return pl.pallas_call(
+        functools.partial(line_kernel, n, pieces, early, row_chunks),
+        out_shape=jax.ShapeDtypeStruct((count, columns), BF16),
+        in_specs=[hbm, vmem, vmem, hbm] + [hbm] * 3,
+        out_specs=vmem,
+        scratch_shapes=[
+            pltpu.VMEM(tokens.shape, BF16),
+            pltpu.VMEM(wo.shape, BF16),
+            dma((3 * pieces + 2,)),
+            pltpu.VMEM((count, span), BF16),
+            pltpu.VMEM((pieces, count, span), BF16),
+            pltpu.VMEM((3, pieces, count, span), BF16),
+            pltpu.VMEM((pieces, n, rows, span), BF16),
+            pltpu.VMEM((n,) + wo.shape, BF16),
+            pltpu.VMEM((4, n // 2, 2 * rows, count), F32),
+            pltpu.VMEM((2, n, rows, count), BF16),
+            pltpu.VMEM((2, n, rows, count), BF16),
+            pltpu.VMEM((2, n, 2, qk_rows, count), BF16),
+            pltpu.VMEM((2, n, qk_rows, count), BF16),
+            pltpu.VMEM((2, n, rows, count), BF16),
+            pltpu.VMEM((2, n, rows, count), BF16),
+            pltpu.VMEM((channels, count), F32),
+            pltpu.VMEM((n, channels, count), BF16),
+            pltpu.VMEM((n, 2, 2, channels, count), BF16),
+            pltpu.VMEM((n, count, 2 * head_width), BF16),
+            pltpu.VMEM((count, columns), F32),
+            dma((n, pieces)),
+            dma((n, pieces)),
+            dma((3, 4, row_chunks)),
+            dma((3, pieces, row_chunks)),
+            dma((n, pieces)),
+            dma((n, pieces)),
+            dma((n, pieces)),
+            dma((n, pieces)),
+            dma((n, pieces)),
+            dma((2, n)),
+            dma((2, n)),
+            dma((2, n)),
+            dma((2, n)),
+            dma((2, n)),
+            dma((2, n)),
+            dma((n,)),
+            dma((n, 3)),
+            dma((n, 2, 2)),
+        ],
+        compiler_params=pltpu.CompilerParams(
+            collective_id=0, has_side_effects=True, vmem_limit_bytes=60 * 1024 * 1024
+        ),
+    )(tokens, norm_gain.reshape(1, -1), head_gain.reshape(1, -1), wo, *shards)
 
 
 def per_device(sizes, tokens, norm_gain, w_query, w_key, w_value, head_gain, w_out):
@@ -523,8 +1108,12 @@
     )
     out_specs = P(("groups", "seq"), ("fsdp", "sub"))
     sizes = (mesh.shape["seq"], mesh.shape["fsdp"], mesh.shape["sub"])
+    if sizes == (4, 2, 2):
+        body = functools.partial(per_device_line, sizes[0])
+    else:
+        body = functools.partial(per_device, sizes)
     return jax.shard_map(
-        functools.partial(per_device, sizes),
+        body,
         mesh=mesh,
         in_specs=in_specs,
         out_specs=out_specs,

time: 100 us -> 88.5 us (0.89)
  Pallas kernels: 97.5 us -> 85.6 us
    pallas_call x1, Pallas kernels: 97.5 us -> 85.6 us  [per_device_line(): pl.pallas_call(functools.partial(line_kernel, n, pieces, early, row_chunk...]
where the time goes in v1:
time: 88.5 us; the launch traced here: 87.9 us
  Pallas kernels  85.6 us (97%)
  local copies, waits for them, and re-layouts  2.3 us (3%)
    pallas_call x1, Pallas kernels, per_device_line(): pl.pallas_call(functools.partial(line_kernel, n, pieces, early, row_chunk...  85.6 us
    unnamed x1, local copies, waits for them, and re-layouts  2.3 us

profile of v1, /device:TPU:0, one launch (start us, length us, event | category | flops | bytes accessed | tf_op | source)
XLA Modules:
  0.0 87.9 jit_solution(2962129488814661212)
XLA Ops:
  0.0 85.6 %shard_map.73 = bf16[256,2048]{1,0:T(8,128)(2,1)} custom-call(bf16[256,8192]{1,0:T(8,128)(2,1)} %tok_hbm.1, f32[1,8192]{1,0:T(1,128)} %bitcast.10, f32[1,128]{1,0:T(1,128)} %bitcast.11, bf16[2,4,32,2048]{3,2,1,0:T(8,128)(2,1)} %bitcast.6, bf16[8,8192]{1,0:T(8,128)(2,1)} %bitcast.8, bf16[8,8192]{1,0:T(8,128)(2,1)} %bitcast.9, bf16[64,8192]{1,0:T(8,128)(2,1)} %bitcast.7), custom_call_target="tpu_custom_call" | custom-call | tf_op jit(solution)/shard_map/pallas_call | solution.py:990
  85.6 2.3 %copy.9 = bf16[256,2048]{1,0:T(8,128)(2,1)} copy(bf16[256,2048]{1,0:T(8,128)(2,1)} %shard_map.73) | data formatting | bytes 2097152

commit v2 on v1

--- a/solution.py
+++ b/solution.py
@@ -455,7 +455,11 @@
 def line_kernel(
     n,
     pieces,
+    w_pieces,
+    out_pieces,
     early,
+    whole_pieces,
+    direct,
     row_chunks,
     tok_hbm,
     gain_ref,
@@ -464,11 +468,14 @@
     wq_hbm,
     wk_hbm,
     wv_hbm,
-    out_ref,
+    out_hbm,
     tok_ref,
     wo_ref,
+    out_ref,
     load_sem,
+    out_sem,
     ysend,
+    ysend2,
     xn,
     xq,
     wall,
@@ -480,6 +487,7 @@
     q_full,
     kv,
     kv_prev,
+    qk_mine,
     nacc,
     num_send,
     num_all,
@@ -503,6 +511,7 @@
     num_s,
     ng_s,
     ng_r,
+    beyond,
 ):
     g = lax.axis_index("groups")
     z = lax.axis_index("seq")
@@ -525,41 +534,63 @@
     p_own = 1 - upper
     p_end = upper
     tokens, width = tok_ref.shape
-    rows, span = wall.shape[2], wall.shape[3]
+    rows, w_span = wall.shape[2], wall.shape[3]
+    span = xn.shape[2]
+    split = span // w_span
     qk_rows = qk.shape[3]
     half_rows = qk_rows // 2
     quarter = f * 2 + s
+    f_other = 1 - f
     q_sib = f * 2 + 1 - s
     q_x = (1 - f) * 2 + s
     q_diag = (1 - f) * 2 + 1 - s
 
     loads = []
-    for c in range(pieces):
+    for c in range(w_pieces):
         row = 0
         for source in (wq_hbm, wk_hbm, wv_hbm):
             size = source.shape[0]
-            col = pl.multiple_of((g * pieces + c) * span, span)
+            col = pl.multiple_of((g * w_pieces + c) * w_span, w_span)
             loads.append(
                 pltpu.make_async_copy(
-                    source.at[:, pl.ds(col, span)],
+                    source.at[:, pl.ds(col, w_span)],
                     wall.at[c, my, pl.ds(row, size)],
-                    load_sem.at[len(loads)],
+                    load_sem.at[c],
                 )
             )
             row += size
-    wo_load = pltpu.make_async_copy(wo_hbm, wo_ref, load_sem.at[len(loads)])
-    tok_load = pltpu.make_async_copy(tok_hbm, tok_ref, load_sem.at[len(loads) + 1])
-    for load in loads + [wo_load, tok_load]:
+
+    def w_loaded(c):
+        slot = wall.at[c, my]
+        pltpu.make_async_copy(slot, slot, load_sem.at[c]).wait()
+
+    wo_load = pltpu.make_async_copy(wo_hbm, wo_ref, load_sem.at[w_pieces])
+    step = tokens // row_chunks
+    tok_loads = [
+        pltpu.make_async_copy(
+            tok_hbm.at[pl.ds(r * step, step)],
+            tok_ref.at[pl.ds(r * step, step)],
+            load_sem.at[w_pieces + 1 + r],
+        )
+        for r in range(row_chunks)
+    ]
+    for load in loads + [wo_load] + tok_loads:
         load.start()
 
     barrier = pltpu.get_barrier_semaphore()
-    for peer in ({"seq": in_z}, {"groups": 1 - g}, {"fsdp": 1 - f}, {"sub": 1 - s}):
+    for peer in (
+        {"seq": in_z},
+        {"groups": 1 - g},
+        {"fsdp": 1 - f},
+        {"sub": 1 - s},
+    ):
         pl.semaphore_signal(barrier, inc=1, device_id=peer, device_id_type=MESH)
 
     @pl.when(inner)
     def _():
         pl.semaphore_signal(barrier, inc=1, device_id={"seq": out_z}, device_id_type=MESH)
         pl.semaphore_wait(barrier, 5)
+        pl.semaphore_signal(beyond, inc=1, device_id={"fsdp": 1 - f}, device_id_type=MESH)
 
     @pl.when(outer)
     def _():
@@ -583,27 +614,30 @@
 
     def w_copy(h, c):
         slot = wall.at[c, h]
-        return remote(slot, slot, w_ss.at[h, c], w_rs.at[h, c], {"seq": in_z})
+        return remote(slot, slot, w_ss.at[h], w_rs.at[h, c], {"seq": in_z})
 
     def o_copy(h, c, own, inward):
         slot = wobuf.at[h, g, c]
         return remote(
             wo_ref.at[g, c] if own else slot,
             slot,
-            (o_in if inward else o_out).at[h, c],
+            (o_in if inward else o_out).at[h],
             o_rs.at[h, c],
             {"seq": in_z if inward else out_z},
         )
 
+    def o_other(c):
+        return remote(
+            wo_ref.at[1 - g, c], wobuf.at[my, 1 - g, c], o_ac.at[my], o_yr.at[my], {"seq": in_z}
+        )
+
     def across(h, c):
         slot = wobuf.at[h, g, c]
-        return remote(slot, slot, o_ac.at[h, c], o_yr.at[h, c], {"groups": 1 - g})
-
-    def crossed(h, c):
-        slot = wobuf.at[h, 1 - g, c]
-        remote(slot, slot, o_ac.at[h, c], o_yr.at[h, c], {"groups": 1 - g}).wait_recv()
-
-    step = tokens // row_chunks
+        return remote(slot, slot, o_ac.at[h], o_yr.at[h], {"groups": 1 - g})
+
+    def crossed(h):
+        slot = wobuf.at[h, 1 - g]
+        remote(slot, slot, o_ac.at[h], o_yr.at[h], {"groups": 1 - g}).wait_recv()
 
     def part_rows(r):
         return pl.ds(r * step, step)
@@ -612,8 +646,17 @@
         return remote(
             ysend.at[part_rows(r)],
             xq.at[0, quarter, part_rows(r)],
-            tok_s.at[0, 0, r],
+            tok_s.at[0, 0],
             tok_r.at[0, quarter, r],
+            {"groups": 1 - g},
+        )
+
+    def y_tok2(r):
+        return remote(
+            ysend2.at[part_rows(r)],
+            xq.at[0, q_x, part_rows(r)],
+            tok_s.at[0, 2],
+            tok_r.at[0, q_x, r],
             {"groups": 1 - g},
         )
 
@@ -622,7 +665,7 @@
         return remote(
             src,
             xq.at[k, quarter, part_rows(r)],
-            tok_s.at[k, 0, r],
+            tok_s.at[k, 0],
             tok_r.at[k, quarter, r],
             {"seq": in_z},
         )
@@ -630,81 +673,106 @@
     def spread_tok(k, c, r, kind):
         slot = xq.at[k, c, part_rows(r)]
         to = {"fsdp": 1 - f} if kind == 2 else {"sub": 1 - s}
-        return remote(slot, slot, tok_s.at[k, kind, r], tok_r.at[k, c, r], to)
+        return remote(slot, slot, tok_s.at[k, kind], tok_r.at[k, c, r], to)
 
     def tok_arrive(k, c, r):
         slot = xq.at[k, c, part_rows(r)]
-        remote(slot, slot, tok_s.at[k, 1, r], tok_r.at[k, c, r], {"sub": 1 - s}).wait_recv()
+        remote(slot, slot, tok_s.at[k, 1], tok_r.at[k, c, r], {"sub": 1 - s}).wait_recv()
 
     def gather_own(k, r):
         tok_arrive(k, quarter, r)
-        launch("inner", spread_tok, k, quarter, r, 2)
-        launch("inner", spread_tok, k, quarter, r, 1)
+        if k > 0 or r < direct:
+            spread_tok(k, quarter, r, 2).start()
+        spread_tok(k, quarter, r, 1).start()
 
     def gather_fwd(k, r):
         tok_arrive(k, q_x, r)
-        launch("inner", spread_tok, k, q_x, r, 3)
+        spread_tok(k, q_x, r, 3).start()
 
     def gathered(k, which):
         for r in range(row_chunks):
             for c in which:
                 tok_arrive(k, c, r)
 
-    def part_copy(p, h):
+    def both(stack):
+        return pl.ds(2 * stack, 2)
+
+    def part_copy(p, stack):
         return remote(
-            part_send.at[p, h],
-            part_recv.at[p, h],
-            part_s.at[p, h],
-            part_r.at[p, h],
+            part_send.at[p, both(stack)],
+            part_recv.at[p, both(stack)],
+            part_s.at[p, stack],
+            part_r.at[p, stack],
             {"groups": 1 - g},
         )
 
-    def qk_copy(p, h):
-        slot = qk.at[p, h, f]
-        return remote(slot, slot, qk_s.at[p, h], qk_r.at[p, h], {"fsdp": 1 - f})
-
-    def qk_arrive(p, h):
-        slot = qk.at[p, h, 1 - f]
-        remote(slot, slot, qk_s.at[p, h], qk_r.at[p, h], {"fsdp": 1 - f}).wait_recv()
-
-    def kv_copy(p, h):
+    def qk_copy(p, stack, way):
+        if way:
+            src = part_send.at[p, both(stack), pl.ds(0, qk_rows)]
+            to = {"groups": 1 - g, "fsdp": 1 - f}
+        else:
+            src, to = qk_mine.at[p, both(stack)], {"fsdp": 1 - f}
         return remote(
-            kv.at[p, h], kv_prev.at[p, h], kv_s.at[p, h], kv_r.at[p, h], {"seq": in_z}
-        )
-
-    def num_copy(h):
+            src, qk.at[p, way, both(stack)], qk_s.at[p, stack, way], qk_r.at[p, stack, way], to
+        )
+
+    def lanes(p):
+        start = p * tokens
+        return pl.ds(start if isinstance(p, int) else pl.multiple_of(start, tokens), tokens)
+
+    def kv_copy(p, stack):
+        there = (both(stack), slice(None), lanes(p))
         return remote(
-            num_send.at[h], num_all.at[h, f, s], num_s.at[h], ng_r.at[h, f, s], {"seq": out_z}
-        )
-
-    def spread_num(h, ff, ss, kind):
-        slot = num_all.at[h, ff, ss]
+            kv.at[there], kv_prev.at[there], kv_s.at[p, stack], kv_r.at[p, stack], {"seq": in_z}
+        )
+
+    def num_copy(stack):
+        return remote(
+            num_send.at[both(stack)],
+            num_all.at[both(stack), f, s],
+            num_s.at[stack],
+            ng_r.at[stack, f, s],
+            {"seq": out_z},
+        )
+
+    def spread_num(stack, kind):
+        ff = f_other if kind == 2 else f
+        slot = num_all.at[both(stack), ff, s]
         to = {"fsdp": 1 - f} if kind == 1 else {"sub": 1 - s}
-        return remote(slot, slot, ng_s.at[h, kind], ng_r.at[h, ff, ss], to)
-
-    def num_arrive(h, ff, ss):
-        slot = num_all.at[h, ff, ss]
-        remote(slot, slot, ng_s.at[h, 0], ng_r.at[h, ff, ss], {"sub": 1 - s}).wait_recv()
+        return remote(slot, slot, ng_s.at[stack, kind], ng_r.at[stack, ff, s], to)
+
+    def num_arrive(stack, ff, ss):
+        slot = num_all.at[both(stack), ff, ss]
+        remote(slot, slot, ng_s.at[stack, 0], ng_r.at[stack, ff, ss], {"sub": 1 - s}).wait_recv()
+
+    def nums_taken(stack):
+        num_arrive(stack, f, s)
+        for kind in (1, 0):
+            spread_num(stack, kind).start()
+
+    def nums_passed(stack):
+        num_arrive(stack, 1 - f, s)
+        spread_num(stack, 2).start()
+
+    def nums_gathered(stack):
+        num_arrive(stack, f, 1 - s)
+        num_arrive(stack, 1 - f, 1 - s)
 
     @pl.when(inner)
     def _():
-        for c in range(pieces):
-            for load in loads[3 * c : 3 * c + 3]:
-                load.wait()
-            launch("inner", w_copy, my, c)
+        for c in range(w_pieces):
+            w_loaded(c)
+            w_copy(my, c).start()
         wo_load.wait()
-        for c in range(pieces):
-            launch("inner", o_copy, my, c, True, False)
+        for c in range(out_pieces):
+            o_copy(my, c, True, False).start()
 
     @pl.when(outer)
     def _():
-        for load in loads:
-            load.wait()
         wo_load.wait()
         for c in range(early):
-            launch("outer", o_copy, my, c, True, True)
-
-    tok_load.wait()
+            o_copy(my, c, True, True).start()
+
     row_step = 16
 
     def norm_rows(i, carry):
@@ -721,18 +789,25 @@
             return (part * scale * gain_ref[:, cols]).astype(BF16)
 
         ysend[block, :] = column((1 - g) * pieces + quarter)
+        ysend2[block, :] = column((1 - g) * pieces + q_x)
         for c in range(pieces):
             xn[c, block, :] = column(g * pieces + c)
         return carry
 
     per_chunk = step // row_step
     for r in range(row_chunks):
+        tok_loads[r].wait()
         lax.fori_loop(r * per_chunk, (r + 1) * per_chunk, norm_rows, 0)
-        launch("all", y_tok, r)
+        y_tok(r).start()
 
         @pl.when(outer)
         def _():
-            launch("outer", z_tok, 1, r)
+            z_tok(1, r).start()
+
+    @pl.when(inner)
+    def _():
+        for r in range(direct, row_chunks):
+            y_tok2(r).start()
 
     def contract(weights, acts):
         return lax.dot_general(weights, acts, (((1,), (1,)), ((), ())), preferred_element_type=F32)
@@ -741,227 +816,308 @@
         if fresh:
             acc[k, stack] = jnp.zeros(acc.shape[2:], F32)
 
-        def body(c, carry):
-            weights = wall[c, 2 * stack : 2 * stack + 2].reshape(2 * rows, span)
-            acts = xn[c] if k == 3 else xq[k, c]
-            acc[k, stack] += contract(weights, acts)
+        def dot(j, i):
+            weights = wall[j * split + i, 2 * stack : 2 * stack + 2].reshape(2 * rows, w_span)
+            where = pl.ds(i * w_span, w_span)
+            return contract(weights, xn[j, :, where] if k == 3 else xq[k, j, :, where])
+
+        def body(j, carry):
+            acc[k, stack] += sum([dot(j, i) for i in range(1, split)], dot(j, 0))
             return carry
 
-        lax.fori_loop(lo, hi, body, 0)
+        lax.fori_loop(lo // split, hi // split, body, 0)
 
     def send_part(k, stack):
         p = p_own if k == 0 else p_end
         for i in range(2):
+            part_send[p, 2 * stack + i] = acc[k, stack, i * rows : (i + 1) * rows].astype(BF16)
+        launch("inner", qk_copy, p, stack, 1)
+        launch("inner", part_copy, p, stack)
+
+    def send_qk(k, stack):
+        p = p_own if k == 3 else p_end
+        for i in range(2):
+            part = acc[k, stack, i * rows : i * rows + qk_rows]
+            qk_mine[p, 2 * stack + i] = part.astype(BF16)
+        launch("inner", qk_copy, p, stack, 0)
+
+    def finish_proj(stack, own):
+        p, k = (p_own, 3) if own else (p_end, 1)
+        part_copy(p, stack).wait_recv()
+        for way in range(2):
+            qk_copy(p, stack, way).wait_recv()
+        for i in range(2):
             h = 2 * stack + i
-            part_send[p, h] = acc[k, stack, i * rows : (i + 1) * rows].astype(BF16)
-            launch("inner", part_copy, p, h)
-
-    def finish_proj(h, own):
-        p, k = (p_own, 3) if own else (p_end, 1)
-        part_copy(p, h).wait_recv()
-        i = h % 2
-        whole = acc[k, h // 2, i * rows : (i + 1) * rows] + part_recv[p, h].astype(F32)
-        qk[p, h, f] = whole[:qk_rows].astype(BF16)
-        kv[p, h, qk_rows:] = whole[qk_rows:].astype(BF16)
-        launch("inner", qk_copy, p, h)
-
-    def finish_qk(h, own):
-        p = p_own if own else p_end
-        qk_arrive(p, h)
-        halves = [qk[p, h, i].astype(F32) for i in range(2)]
-        q_full[p, h] = jnp.concatenate([x[:half_rows] for x in halves], 0).astype(BF16)
-        kv[p, h, :qk_rows] = jnp.concatenate([x[half_rows:] for x in halves], 0).astype(BF16)
+            whole = acc[k, stack, i * rows : (i + 1) * rows] + part_recv[p, h].astype(F32)
+            mine = whole[:qk_rows].astype(BF16).astype(F32)
+            other = qk[p, 0, h].astype(F32) + qk[p, 1, h].astype(F32)
+            lower = jnp.where(f == 0, mine, other)
+            higher = jnp.where(f == 0, other, mine)
+
+            def dims(first):
+                last = first + half_rows
+                return jnp.concatenate([lower[first:last], higher[first:last]], 0).astype(BF16)
+
+            q_full[h, pl.ds(0, qk_rows), lanes(p)] = dims(0)
+            kv[h, pl.ds(0, qk_rows), lanes(p)] = dims(half_rows)
+            kv[h, pl.ds(qk_rows, rows - qk_rows), lanes(p)] = whole[qk_rows:].astype(BF16)
 
         @pl.when(low)
         def _():
-            launch("low", kv_copy, p, h)
-
-    key_pos = lax.broadcasted_iota(jnp.int32, (tokens, tokens), 0)
-    query_pos = lax.broadcasted_iota(jnp.int32, (tokens, tokens), 1)
-
-    def attend_to(source, queries, diagonal):
+            launch("low", kv_copy, p, stack)
+
+    def attend_to(source, queries, causal):
         scores = lax.dot_general(
             source[:qk_rows], queries, (((0,), (0,)), ((), ())), preferred_element_type=F32
         )
         value = 1.0 + scores * 0.25 + scores * scores * 0.03125
-        if diagonal:
+        if causal:
+            key_pos = lax.broadcasted_iota(jnp.int32, value.shape, 0)
+            query_pos = lax.broadcasted_iota(jnp.int32, value.shape, 1)
             value = jnp.where(key_pos <= query_pos, value, 0.0)
         return jnp.dot(source[qk_rows:], value.astype(BF16), preferred_element_type=F32)
 
-    def prior_arrive(h):
-        for p in range(2):
-            kv_copy(p, h).wait_recv()
-
-    def numerator(h, own):
-        p = p_own if own else p_end
-        queries = q_full[p, h]
-        nacc[...] = attend_to(kv[p, h], queries, True)
-
-        @pl.when(low if own else high)
-        def _():
-            nacc[...] += attend_to(kv[1 - p, h], queries, False)
-
+    def attend_own(stack):
+        for i in range(2):
+            h = 2 * stack + i
+            nacc[i] = attend_to(kv[h], q_full[h], True)
+
+    def attend_prior(stack):
         @pl.when(high)
         def _():
-            nacc[...] += attend_to(kv_prev[0, h], queries, False) + attend_to(
-                kv_prev[1, h], queries, False
-            )
-
-        if own:
-            num_all[h, f, s] = nacc[...].astype(BF16)
-            launch("inner", spread_num, h, f, s, 1)
-            launch("inner", spread_num, h, f, s, 0)
-        else:
-            num_send[h] = nacc[...].astype(BF16)
-            launch("inner", num_copy, h)
-
-    def o_relay(role, h, c, inward):
-        o_copy(h, c, False, True).wait_recv()
-        if inward is not None:
-            launch(role, o_copy, h, c, False, inward)
-        launch(role, across, h, c)
+            for p in (p_own, p_end):
+                kv_copy(p, stack).wait_recv()
+            for i in range(2):
+                h = 2 * stack + i
+                nacc[i] += attend_to(kv_prev[h], q_full[h], False)
+
+        for i in range(2):
+            num_send[2 * stack + i] = nacc.at[i][:, lanes(p_end)].astype(BF16)
+        launch("inner", num_copy, stack)
+        for i in range(2):
+            num_all[2 * stack + i, f, s] = nacc.at[i][:, lanes(p_own)].astype(BF16)
+
+    def spread_nums(stack):
+        for kind in (1, 0):
+            spread_num(stack, kind).start()
+
+    def o_relay(h, pieces_now, inward, cross=True):
+        for c in pieces_now:
+            o_copy(h, c, False, True).wait_recv()
+            if inward is not None:
+                o_copy(h, c, False, inward).start()
+            if cross and not (inward and c >= out_pieces - whole_pieces):
+                across(h, c).start()
 
     def w_relay(c):
         w_copy(sl_out, c).wait_recv()
-        launch("inner", w_copy, sl_out, c)
-
-    late = range(early, pieces)
-
-    @pl.when(inner)
-    def _():
-        for c in range(pieces):
-            launch("inner", o_copy, my, c, True, True)
-        for c in range(early):
-            o_relay("inner", sl_out, c, True)
-        gather_own(0, 0)
-        gather_own(1, 0)
-        gather_own(0, 1)
-        for c in range(pieces):
-            w_copy(second, c).wait_recv()
-        project(3, 0, 0, pieces, True)
-        gather_fwd(0, 0)
-        gather_own(1, 1)
-        for c in range(2):
-            o_relay("inner", second, c, False)
-        gather_fwd(1, 0)
-        gather_own(2, 0)
-        for c in range(2, pieces):
-            o_relay("inner", second, c, False)
-        gather_fwd(0, 1)
-        gathered(0, (q_sib, q_diag))
-        project(0, 0, 0, pieces, True)
-        send_part(0, 0)
-        gather_own(2, 1)
-        for c in range(early):
-            o_relay("inner", sl_far, c, False)
-        w_relay(0)
-        gather_fwd(1, 1)
-        gathered(1, (q_sib, q_diag))
-        project(1, 0, 0, pieces, True)
-        w_relay(1)
-        for h in range(2):
-            finish_proj(h, True)
-        gather_fwd(2, 0)
-        w_relay(2)
-        w_relay(3)
-        for h in range(2):
-            finish_qk(h, True)
-        gather_fwd(2, 1)
-        gathered(2, (q_sib, q_diag))
-        project(2, 0, 0, pieces, True)
-        send_part(2, 0)
-        for c in range(pieces - 1):
-            w_copy(sl_far, c).wait_recv()
-        for k in range(4):
-            project(k, 1, 0, pieces - 1, True)
-        for c in late:
-            o_relay("inner", sl_out, c, True)
-        for h in range(2):
-            finish_proj(h, False)
-        w_copy(sl_far, pieces - 1).wait_recv()
-        for k in (2, 0):
-            project(k, 1, pieces - 1, pieces, False)
-            send_part(k, 1)
-        for k in (3, 1):
-            project(k, 1, pieces - 1, pieces, False)
-        for h in range(2):
-            finish_qk(h, False)
-
-        def attention(h):
-            @pl.when(high)
-            def _():
-                prior_arrive(h)
-
-            numerator(h, False)
-            numerator(h, True)
-
-        for h in range(2):
-            attention(h)
-        for c in late:
-            o_relay("inner", sl_far, c, False)
-        for h in range(2, 4):
-            finish_proj(h, False)
-            finish_proj(h, True)
-        for h in range(2, 4):
-            finish_qk(h, False)
-            finish_qk(h, True)
-        for h in range(2, 4):
-            attention(h)
-
-    @pl.when(outer)
-    def _():
-        for r in range(row_chunks):
-            tok_arrive(0, quarter, r)
-            launch("outer", z_tok, 2, r)
-        for c in range(pieces):
-            launch("outer", w_copy, my, c)
-        for c in late:
-            launch("outer", o_copy, my, c, True, True)
-        for h in (near, second):
-            for c in range(pieces):
-                o_relay("outer", h, c, None)
-        for c in range(pieces):
-            o_relay("outer", sl_far, c, None)
-        for h in range(n):
-            num_arrive(h, f, s)
-            launch("outer", spread_num, h, f, s, 1)
-            launch("outer", spread_num, h, f, s, 0)
+        w_copy(sl_out, c).start()
 
     head_width = 2 * num_all.shape[3]
     columns = out_ref.shape[1]
     depth = 2 * head_width
 
     def attend_block(h):
-        num_arrive(h, 1 - f, s)
-        launch("all", spread_num, h, 1 - f, s, 2)
-        num_arrive(h, f, 1 - s)
-        num_arrive(h, 1 - f, 1 - s)
         for i in range(2):
             whole = jnp.concatenate([num_all[h, j, i] for j in range(2)], 0).astype(F32)
             meansq = jnp.sum(whole * whole, axis=0, keepdims=True) / head_width
             scaled = (whole * lax.rsqrt(meansq + 1e-06)).T * head_gain_ref[...]
             attended[h, :, i * head_width : (i + 1) * head_width] = scaled.astype(BF16)
 
+    def out_copy(r):
+        block = part_rows(r)
+        return pltpu.make_async_copy(out_ref.at[block], out_hbm.at[block], out_sem.at[r])
+
     def multiply(h):
+        def add(weights):
+            weights = weights.reshape(depth, columns)
+            if h == 0:
+                total[...] = jnp.dot(attended[h], weights, preferred_element_type=F32)
+            elif h < n - 1:
+                total[...] += jnp.dot(attended[h], weights, preferred_element_type=F32)
+            else:
+                for r in range(row_chunks):
+                    block = part_rows(r)
+                    product = jnp.dot(attended[h, block], weights, preferred_element_type=F32)
+                    out_ref[block] = (total[block] + product).astype(BF16)
+                    out_copy(r).start()
+
         @pl.when(my == h)
         def _():
-            total[...] += jnp.dot(
-                attended[h], wo_ref[...].reshape(depth, columns), preferred_element_type=F32
-            )
+            add(wo_ref[...])
 
         @pl.when(my != h)
         def _():
-            for c in range(pieces):
-                crossed(h, c)
-            total[...] += jnp.dot(
-                attended[h], wobuf[h].reshape(depth, columns), preferred_element_type=F32
-            )
-
-    total[...] = jnp.zeros(total.shape, F32)
-    for h in range(n):
-        attend_block(h)
-        multiply(h)
-    out_ref[...] = total[...].astype(BF16)
+            crossed(h)
+            add(wobuf[h])
+
+    late = range(early, out_pieces)
+    def far_w(c):
+        w_copy(sl_far, c).wait_recv()
+
+    @pl.when(inner)
+    def _():
+        for c in range(out_pieces):
+            o_copy(my, c, True, True).start()
+        o_relay(sl_out, range(early), True)
+        gather_own(0, 0)
+        gather_own(1, 0)
+        gather_own(0, 1)
+        gather_fwd(0, 0)
+        gather_own(1, 1)
+        gather_own(0, 2)
+        gather_fwd(1, 0)
+        gather_own(1, 2)
+        gather_own(0, 3)
+        for c in range(w_pieces):
+            w_copy(second, c).wait_recv()
+        project(3, 0, 0, w_pieces, True)
+        send_qk(3, 0)
+        gather_fwd(0, 1)
+        gather_own(1, 3)
+        gather_fwd(0, 2)
+        o_relay(second, (0, 1), False)
+        gather_fwd(1, 1)
+        gather_own(2, 0)
+        gather_fwd(0, 3)
+        o_relay(second, (2, 3), False)
+        gather_fwd(1, 2)
+        gather_own(2, 1)
+        o_relay(second, (4, 5), False)
+        gather_fwd(1, 3)
+        gather_own(2, 2)
+        gathered(0, (q_sib, q_diag))
+        project(0, 0, 0, w_pieces, True)
+        pl.semaphore_wait(beyond, 1)
+        send_part(0, 0)
+        o_relay(second, (6, 7), False)
+        gather_fwd(2, 0)
+        gather_own(2, 3)
+        gathered(1, (q_sib, q_diag))
+        project(1, 0, 0, w_pieces, True)
+        send_qk(1, 0)
+        o_relay(sl_far, range(early), False)
+        gather_fwd(2, 1)
+        w_relay(0)
+        w_relay(1)
+        gather_fwd(2, 2)
+        w_relay(2)
+        w_relay(3)
+        gather_fwd(2, 3)
+        gathered(2, (q_sib, q_diag))
+        project(2, 0, 0, w_pieces, True)
+        send_part(2, 0)
+        w_relay(4)
+        w_relay(5)
+        far_w(0)
+        far_w(1)
+        for k in range(4):
+            project(k, 1, 0, 2, True)
+        w_relay(6)
+        far_w(2)
+        far_w(3)
+        for k in range(4):
+            project(k, 1, 2, 4, False)
+        w_relay(7)
+        finish_proj(0, True)
+        far_w(4)
+        far_w(5)
+        for k in range(4):
+            project(k, 1, 4, 6, False)
+        finish_proj(0, False)
+        o_relay(sl_out, (early, early + 1), True, False)
+        far_w(6)
+        o_relay(sl_out, (early + 2,), True, False)
+        far_w(7)
+        for k in (2, 0):
+            project(k, 1, 6, w_pieces, False)
+            send_part(k, 1)
+        for c in range(early, min(early + 3, out_pieces - whole_pieces)):
+            across(sl_out, c).start()
+        for k in (1, 3):
+            project(k, 1, 6, w_pieces, False)
+            send_qk(k, 1)
+        o_relay(sl_out, range(early + 3, out_pieces), True)
+        attend_own(0)
+        o_relay(sl_far, (early, early + 1), False)
+        attend_prior(0)
+        finish_proj(1, False)
+        finish_proj(1, True)
+        spread_nums(0)
+        o_relay(sl_far, range(early + 2, early + 4), False)
+        attend_own(1)
+
+        @pl.when(high)
+        def _():
+            o_relay(sl_far, range(early + 4, out_pieces), False)
+
+        attend_prior(1)
+        spread_nums(1)
+
+        @pl.when(low)
+        def _():
+            o_relay(sl_far, range(early + 4, out_pieces), False)
+
+        nums_passed(0)
+        nums_gathered(0)
+        for h in range(2):
+            attend_block(h)
+            multiply(h)
+        nums_passed(1)
+        nums_gathered(1)
+        for h in range(2, n):
+            attend_block(h)
+            multiply(h)
+
+    @pl.when(outer)
+    def _():
+        for r in range(row_chunks):
+            tok_arrive(0, quarter, r)
+            z_tok(2, r).start()
+        for c in range(w_pieces):
+            w_loaded(c)
+            w_copy(my, c).start()
+        for c in late:
+            o_copy(my, c, True, True).start()
+        for c in range(out_pieces - whole_pieces, out_pieces):
+            o_other(c).start()
+        o_relay(near, range(out_pieces), None)
+        o_relay(second, range(out_pieces), None)
+        o_relay(sl_far, range(early), None)
+        nums_taken(0)
+        o_relay(sl_far, range(early, early + 2), None)
+        nums_passed(0)
+
+        @pl.when(low)
+        def _():
+            o_relay(sl_far, range(early + 2, early + 4), None)
+            nums_taken(1)
+
+        nums_gathered(0)
+        for h in range(2):
+            attend_block(h)
+            multiply(h)
+
+        @pl.when(high)
+        def _():
+            o_relay(sl_far, range(early + 2, out_pieces), None)
+            nums_taken(1)
+
+        @pl.when(low)
+        def _():
+            o_relay(sl_far, range(early + 4, out_pieces), None)
+
+        nums_passed(1)
+        nums_gathered(1)
+        for h in range(2, n):
+            attend_block(h)
+            multiply(h)
+
+    def flush(whole, sem):
+        remote(whole, whole, sem, sem, {"sub": 1 - s}).wait_send()
+
+    def tok_flush(k, kind):
+        flush(xq.at[k, quarter], tok_s.at[k, kind])
 
     for role, gate in (("inner", inner), ("outer", outer), ("low", inner & low)):
 
@@ -970,8 +1126,36 @@
             for make, args in logs[role]:
                 make(*args).wait_send()
 
-    for make, args in logs["all"]:
-        make(*args).wait_send()
+    @pl.when(inner)
+    def _():
+        for h in (my, sl_out):
+            flush(wall.at[:, h], w_ss.at[h])
+            flush(wobuf.at[h, g], o_in.at[h])
+        for h in (my, second, sl_far):
+            flush(wobuf.at[h, g], o_out.at[h])
+        for h in (second, sl_far):
+            flush(wobuf.at[h, g], o_ac.at[h])
+        flush(wobuf.at[sl_out, g, pl.ds(0, out_pieces - whole_pieces)], o_ac.at[sl_out])
+        for k in range(3):
+            for kind in (1, 2, 3):
+                tok_flush(k, kind)
+
+    @pl.when(outer)
+    def _():
+        flush(wall.at[:, my], w_ss.at[my])
+        flush(wobuf.at[my, g], o_in.at[my])
+        for h in (near, second, sl_far):
+            flush(wobuf.at[h, g], o_ac.at[h])
+        flush(wobuf.at[my, g, pl.ds(0, whole_pieces)], o_ac.at[my])
+        for k in (1, 2):
+            tok_flush(k, 0)
+
+    tok_flush(0, 0)
+    for stack in range(2):
+        for kind in range(3):
+            spread_num(stack, kind).wait_send()
+    for r in range(row_chunks):
+        out_copy(r).wait()
 
 
 def per_device_line(n, tokens, norm_gain, w_query, w_key, w_value, head_gain, w_out):
@@ -981,56 +1165,62 @@
     qk_rows = w_query.shape[1] + w_key.shape[1]
     channels = w_value.shape[1]
     head_width, columns = w_out.shape[1], w_out.shape[2]
-    pieces, early, row_chunks = 4, 2, 2
+    pieces, w_pieces, out_pieces, row_chunks = 4, 8, 8, 4
+    early, whole_pieces, direct = 3, 3, 2
     span = width // (2 * pieces)
-    wo = w_out.reshape(2, pieces, head_width // pieces, columns)
+    wo = w_out.reshape(2, out_pieces, head_width // out_pieces, columns)
     hbm = pl.BlockSpec(memory_space=pl.ANY)
     vmem = pl.BlockSpec(memory_space=pltpu.VMEM)
     dma = pltpu.SemaphoreType.DMA
     return pl.pallas_call(
-        functools.partial(line_kernel, n, pieces, early, row_chunks),
+        functools.partial(line_kernel, n, pieces, w_pieces, out_pieces, early, whole_pieces, direct, row_chunks),
         out_shape=jax.ShapeDtypeStruct((count, columns), BF16),
         in_specs=[hbm, vmem, vmem, hbm] + [hbm] * 3,
-        out_specs=vmem,
+        out_specs=hbm,
         scratch_shapes=[
             pltpu.VMEM(tokens.shape, BF16),
             pltpu.VMEM(wo.shape, BF16),
-            dma((3 * pieces + 2,)),
+            pltpu.VMEM((count, columns), BF16),
+            dma((w_pieces + 1 + row_chunks,)),
+            dma((row_chunks,)),
+            pltpu.VMEM((count, span), BF16),
             pltpu.VMEM((count, span), BF16),
             pltpu.VMEM((pieces, count, span), BF16),
             pltpu.VMEM((3, pieces, count, span), BF16),
-            pltpu.VMEM((pieces, n, rows, span), BF16),
+            pltpu.VMEM((w_pieces, n, rows, span * pieces // w_pieces), BF16),
             pltpu.VMEM((n,) + wo.shape, BF16),
             pltpu.VMEM((4, n // 2, 2 * rows, count), F32),
             pltpu.VMEM((2, n, rows, count), BF16),
             pltpu.VMEM((2, n, rows, count), BF16),
-            pltpu.VMEM((2, n, 2, qk_rows, count), BF16),
+            pltpu.VMEM((2, 2, n, qk_rows, count), BF16),
+            pltpu.VMEM((n, qk_rows, 2 * count), BF16),
+            pltpu.VMEM((n, rows, 2 * count), BF16),
+            pltpu.VMEM((n, rows, 2 * count), BF16),
             pltpu.VMEM((2, n, qk_rows, count), BF16),
-            pltpu.VMEM((2, n, rows, count), BF16),
-            pltpu.VMEM((2, n, rows, count), BF16),
-            pltpu.VMEM((channels, count), F32),
+            pltpu.VMEM((2, channels, 2 * count), F32),
             pltpu.VMEM((n, channels, count), BF16),
             pltpu.VMEM((n, 2, 2, channels, count), BF16),
             pltpu.VMEM((n, count, 2 * head_width), BF16),
             pltpu.VMEM((count, columns), F32),
-            dma((n, pieces)),
-            dma((n, pieces)),
-            dma((3, 4, row_chunks)),
+            dma((n,)),
+            dma((n, w_pieces)),
+            dma((3, 4)),
             dma((3, pieces, row_chunks)),
-            dma((n, pieces)),
-            dma((n, pieces)),
-            dma((n, pieces)),
-            dma((n, pieces)),
-            dma((n, pieces)),
-            dma((2, n)),
-            dma((2, n)),
-            dma((2, n)),
-            dma((2, n)),
-            dma((2, n)),
-            dma((2, n)),
             dma((n,)),
-            dma((n, 3)),
-            dma((n, 2, 2)),
+            dma((n,)),
+            dma((n, out_pieces)),
+            dma((n,)),
+            dma((n,)),
+            dma((2, n // 2)),
+            dma((2, n // 2)),
+            dma((2, n // 2, 2)),
+            dma((2, n // 2, 2)),
+            dma((2, n // 2)),
+            dma((2, n // 2)),
+            dma((n // 2,)),
+            dma((n // 2, 3)),
+            dma((n // 2, 2, 2)),
+            pltpu.SemaphoreType.REGULAR,
         ],
         compiler_params=pltpu.CompilerParams(
             collective_id=0, has_side_effects=True, vmem_limit_bytes=60 * 1024 * 1024

time: 88.5 us -> 79 us (0.89)
  the two profiles are of different devices: /device:TPU:0 before, /device:TPU:25 now
where the time goes in v2:
time: 79 us; the launch traced here: 78.7 us
  Pallas kernels  76.4 us (97%)
  local copies, waits for them, and re-layouts  2.3 us (3%)
    pallas_call x1, Pallas kernels, per_device_line(): pl.pallas_call(functools.partial(line_kernel, n, pieces, w_pieces, out_pi...  76.4 us
    unnamed x1, local copies, waits for them, and re-layouts  2.3 us

profile of v2, /device:TPU:25, one launch (start us, length us, event | category | flops | bytes accessed | tf_op | source)
XLA Modules:
  0.0 78.7 jit_solution(11681767101950647853)
XLA Ops:
  0.0 76.4 %shard_map.73 = bf16[256,2048]{1,0:T(8,128)(2,1)} custom-call(bf16[256,8192]{1,0:T(8,128)(2,1)} %tok_hbm.1, f32[1,8192]{1,0:T(1,128)} %bitcast.10, f32[1,128]{1,0:T(1,128)} %bitcast.11, bf16[2,8,16,2048]{3,2,1,0:T(8,128)(2,1)} %bitcast.6, bf16[8,8192]{1,0:T(8,128)(2,1)} %bitcast.8, bf16[8,8192]{1,0:T(8,128)(2,1)} %bitcast.9, bf16[64,8192]{1,0:T(8,128)(2,1)} %bitcast.7), custom_call_target="tpu_custom_call" | custom-call | tf_op jit(solution)/shard_map/pallas_call | solution.py:1175
  76.4 2.3 %copy.9 = bf16[256,2048]{1,0:T(8,128)(2,1)} copy(bf16[256,2048]{1,0:T(8,128)(2,1)} %shard_map.73) | data formatting | bytes 2097152

commit v3 on v2

--- a/solution.py
+++ b/solution.py
@@ -486,7 +486,9 @@
     qk,
     q_full,
     kv,
-    kv_prev,
+    state,
+    state_in,
+    feats,
     qk_mine,
     nacc,
     num_send,
@@ -720,10 +722,13 @@
         start = p * tokens
         return pl.ds(start if isinstance(p, int) else pl.multiple_of(start, tokens), tokens)
 
-    def kv_copy(p, stack):
-        there = (both(stack), slice(None), lanes(p))
+    def state_copy(stack):
         return remote(
-            kv.at[there], kv_prev.at[there], kv_s.at[p, stack], kv_r.at[p, stack], {"seq": in_z}
+            state.at[both(stack)],
+            state_in.at[both(stack)],
+            kv_s.at[stack],
+            kv_r.at[stack],
+            {"seq": in_z},
         )
 
     def num_copy(stack):
@@ -854,17 +859,13 @@
             lower = jnp.where(f == 0, mine, other)
             higher = jnp.where(f == 0, other, mine)
 
-            def dims(first):
+            def joined(first):
                 last = first + half_rows
                 return jnp.concatenate([lower[first:last], higher[first:last]], 0).astype(BF16)
 
-            q_full[h, pl.ds(0, qk_rows), lanes(p)] = dims(0)
-            kv[h, pl.ds(0, qk_rows), lanes(p)] = dims(half_rows)
+            q_full[h, pl.ds(0, qk_rows), lanes(p)] = joined(0)
+            kv[h, pl.ds(0, qk_rows), lanes(p)] = joined(half_rows)
             kv[h, pl.ds(qk_rows, rows - qk_rows), lanes(p)] = whole[qk_rows:].astype(BF16)
-
-        @pl.when(low)
-        def _():
-            launch("low", kv_copy, p, stack)
 
     def attend_to(source, queries, causal):
         scores = lax.dot_general(
@@ -877,7 +878,38 @@
             value = jnp.where(key_pos <= query_pos, value, 0.0)
         return jnp.dot(source[qk_rows:], value.astype(BF16), preferred_element_type=F32)
 
+    dims = qk_rows
+    sub = dims // 2
+    used = sub * dims + sub * sub + dims
+
+    def features(vectors):
+        x = vectors.astype(F32)
+        parts = [x * x[i : i + 1] for i in range(sub)]
+        parts += [x[sub:] * x[i : i + 1] for i in range(sub, dims)]
+        rest = (feats.shape[1] - used, x.shape[1])
+        one = lax.broadcasted_iota(jnp.int32, rest, 0) == 0
+        return jnp.concatenate(parts + [x, jnp.where(one, 1.0, 0.0)], 0).astype(BF16)
+
+    def send_state(stack):
+        @pl.when(low)
+        def _():
+            col = lax.broadcasted_iota(jnp.int32, (1, state.shape[2]), 1)
+            twice = (col < sub * dims) & (col % dims >= sub)
+            factor = jnp.where(twice, 0.0625, 0.03125)
+            factor = jnp.where(col >= used - dims, 0.25, factor)
+            factor = jnp.where(col >= used, 1.0, factor)
+            for h in range(2 * stack, 2 * stack + 2):
+                block = kv[h]
+                sums = contract(block[qk_rows:], features(block[:qk_rows]))
+                state[h] = (sums * factor).astype(BF16)
+            launch("low", state_copy, stack)
+
     def attend_own(stack):
+        @pl.when(high)
+        def _():
+            for i in range(2):
+                feats[i] = features(q_full[2 * stack + i])
+
         for i in range(2):
             h = 2 * stack + i
             nacc[i] = attend_to(kv[h], q_full[h], True)
@@ -885,11 +917,10 @@
     def attend_prior(stack):
         @pl.when(high)
         def _():
-            for p in (p_own, p_end):
-                kv_copy(p, stack).wait_recv()
+            state_copy(stack).wait_recv()
             for i in range(2):
                 h = 2 * stack + i
-                nacc[i] += attend_to(kv_prev[h], q_full[h], False)
+                nacc[i] += jnp.dot(state_in[h], feats[i], preferred_element_type=F32)
 
         for i in range(2):
             num_send[2 * stack + i] = nacc.at[i][:, lanes(p_end)].astype(BF16)
@@ -924,32 +955,27 @@
             scaled = (whole * lax.rsqrt(meansq + 1e-06)).T * head_gain_ref[...]
             attended[h, :, i * head_width : (i + 1) * head_width] = scaled.astype(BF16)
 
+    out_span = columns // row_chunks
+
     def out_copy(r):
-        block = part_rows(r)
-        return pltpu.make_async_copy(out_ref.at[block], out_hbm.at[block], out_sem.at[r])
-
-    def multiply(h):
-        def add(weights):
-            weights = weights.reshape(depth, columns)
-            if h == 0:
-                total[...] = jnp.dot(attended[h], weights, preferred_element_type=F32)
-            elif h < n - 1:
-                total[...] += jnp.dot(attended[h], weights, preferred_element_type=F32)
-            else:
-                for r in range(row_chunks):
-                    block = part_rows(r)
-                    product = jnp.dot(attended[h, block], weights, preferred_element_type=F32)
-                    out_ref[block] = (total[block] + product).astype(BF16)
-                    out_copy(r).start()
-
-        @pl.when(my == h)
-        def _():
-            add(wo_ref[...])
-
-        @pl.when(my != h)
-        def _():
+        block = pl.ds(r * out_span, out_span)
+        return pltpu.make_async_copy(out_ref.at[:, block], out_hbm.at[:, block], out_sem.at[r])
+
+    def multiply(h, own, first=False, last=False):
+        attend_block(h)
+        if not own:
             crossed(h)
-            add(wobuf[h])
+        weights = (wo_ref[...] if own else wobuf[h]).reshape(depth, columns)
+        if first:
+            total[...] = jnp.dot(attended[h], weights, preferred_element_type=F32)
+        elif not last:
+            total[...] += jnp.dot(attended[h], weights, preferred_element_type=F32)
+        else:
+            for r in range(row_chunks):
+                block = slice(r * out_span, (r + 1) * out_span)
+                product = jnp.dot(attended[h], weights[:, block], preferred_element_type=F32)
+                out_ref[:, block] = (total[:, block] + product).astype(BF16)
+                out_copy(r).start()
 
     late = range(early, out_pieces)
     def far_w(c):
@@ -1025,6 +1051,7 @@
         for k in range(4):
             project(k, 1, 4, 6, False)
         finish_proj(0, False)
+        send_state(0)
         o_relay(sl_out, (early, early + 1), True, False)
         far_w(6)
         o_relay(sl_out, (early + 2,), True, False)
@@ -1042,9 +1069,10 @@
         o_relay(sl_far, (early, early + 1), False)
         attend_prior(0)
         finish_proj(1, False)
+        o_relay(sl_far, range(early + 2, early + 4), False)
         finish_proj(1, True)
+        send_state(1)
         spread_nums(0)
-        o_relay(sl_far, range(early + 2, early + 4), False)
         attend_own(1)
 
         @pl.when(high)
@@ -1060,14 +1088,12 @@
 
         nums_passed(0)
         nums_gathered(0)
-        for h in range(2):
-            attend_block(h)
-            multiply(h)
+        multiply(my, True, first=True)
+        multiply(second, False)
         nums_passed(1)
         nums_gathered(1)
-        for h in range(2, n):
-            attend_block(h)
-            multiply(h)
+        multiply(sl_out, False)
+        multiply(sl_far, False, last=True)
 
     @pl.when(outer)
     def _():
@@ -1086,6 +1112,11 @@
         o_relay(sl_far, range(early), None)
         nums_taken(0)
         o_relay(sl_far, range(early, early + 2), None)
+
+        @pl.when(high)
+        def _():
+            o_relay(sl_far, range(early + 2, early + 4), None)
+
         nums_passed(0)
 
         @pl.when(low)
@@ -1093,25 +1124,27 @@
             o_relay(sl_far, range(early + 2, early + 4), None)
             nums_taken(1)
 
-        nums_gathered(0)
-        for h in range(2):
-            attend_block(h)
-            multiply(h)
-
         @pl.when(high)
         def _():
-            o_relay(sl_far, range(early + 2, out_pieces), None)
-            nums_taken(1)
+            o_relay(sl_far, range(early + 4, out_pieces), None)
+
+        nums_gathered(0)
+        multiply(near, False, first=True)
 
         @pl.when(low)
         def _():
             o_relay(sl_far, range(early + 4, out_pieces), None)
 
+        multiply(second, False)
+
+        @pl.when(high)
+        def _():
+            nums_taken(1)
+
         nums_passed(1)
         nums_gathered(1)
-        for h in range(2, n):
-            attend_block(h)
-            multiply(h)
+        multiply(my, True)
+        multiply(sl_far, False, last=True)
 
     def flush(whole, sem):
         remote(whole, whole, sem, sem, {"sub": 1 - s}).wait_send()
@@ -1168,6 +1201,8 @@
     pieces, w_pieces, out_pieces, row_chunks = 4, 8, 8, 4
     early, whole_pieces, direct = 3, 3, 2
     span = width // (2 * pieces)
+    products = qk_rows * qk_rows * 3 // 4 + qk_rows + 1
+    feature_rows = -(-products // 128) * 128
     wo = w_out.reshape(2, out_pieces, head_width // out_pieces, columns)
     hbm = pl.BlockSpec(memory_space=pl.ANY)
     vmem = pl.BlockSpec(memory_space=pltpu.VMEM)
@@ -1195,7 +1230,9 @@
             pltpu.VMEM((2, 2, n, qk_rows, count), BF16),
             pltpu.VMEM((n, qk_rows, 2 * count), BF16),
             pltpu.VMEM((n, rows, 2 * count), BF16),
-            pltpu.VMEM((n, rows, 2 * count), BF16),
+            pltpu.VMEM((n, channels, feature_rows), BF16),
+            pltpu.VMEM((n, channels, feature_rows), BF16),
+            pltpu.VMEM((2, feature_rows, 2 * count), BF16),
             pltpu.VMEM((2, n, qk_rows, count), BF16),
             pltpu.VMEM((2, channels, 2 * count), F32),
             pltpu.VMEM((n, channels, count), BF16),
@@ -1215,8 +1252,8 @@
             dma((2, n // 2)),
             dma((2, n // 2, 2)),
             dma((2, n // 2, 2)),
-            dma((2, n // 2)),
-            dma((2, n // 2)),
+            dma((n // 2,)),
+            dma((n // 2,)),
             dma((n // 2,)),
             dma((n // 2, 3)),
             dma((n // 2, 2, 2)),

time: 79 us -> 77.6 us (0.982)
  the two profiles are of different devices: /device:TPU:25 before, /device:TPU:0 now
where the time goes in v3:
time: 77.6 us; the launch traced here: 77.4 us
  Pallas kernels  75.1 us (97%)
  local copies, waits for them, and re-layouts  2.3 us (3%)
    pallas_call x1, Pallas kernels, per_device_line(): pl.pallas_call(functools.partial(line_kernel, n, pieces, w_pieces, out_pi...  75.1 us
    unnamed x1, local copies, waits for them, and re-layouts  2.3 us

profile of v3, /device:TPU:0, one launch (start us, length us, event | category | flops | bytes accessed | tf_op | source)
XLA Modules:
  0.0 77.4 jit_solution(18117880733727679359)
XLA Ops:
  0.0 75.1 %shard_map.73 = bf16[256,2048]{1,0:T(8,128)(2,1)} custom-call(bf16[256,8192]{1,0:T(8,128)(2,1)} %tok_hbm.1, f32[1,8192]{1,0:T(1,128)} %bitcast.10, f32[1,128]{1,0:T(1,128)} %bitcast.11, bf16[2,8,16,2048]{3,2,1,0:T(8,128)(2,1)} %bitcast.6, bf16[8,8192]{1,0:T(8,128)(2,1)} %bitcast.8, bf16[8,8192]{1,0:T(8,128)(2,1)} %bitcast.9, bf16[64,8192]{1,0:T(8,128)(2,1)} %bitcast.7), custom_call_target="tpu_custom_call" | custom-call | tf_op jit(solution)/shard_map/pallas_call | solution.py:1210
  75.1 2.3 %copy.9 = bf16[256,2048]{1,0:T(8,128)(2,1)} copy(bf16[256,2048]{1,0:T(8,128)(2,1)} %shard_map.73) | data formatting | bytes 2097152

commit v4 on v3

--- a/solution.py
+++ b/solution.py
@@ -499,6 +499,8 @@
     w_rs,
     tok_s,
     tok_r,
+    tok_x,
+    tok_w,
     o_out,
     o_in,
     o_rs,
@@ -576,8 +578,16 @@
         )
         for r in range(row_chunks)
     ]
-    for load in loads + [wo_load] + tok_loads:
-        load.start()
+
+    @pl.when(inner)
+    def _():
+        for load in loads + tok_loads + [wo_load]:
+            load.start()
+
+    @pl.when(outer)
+    def _():
+        for load in [wo_load] + tok_loads + loads:
+            load.start()
 
     barrier = pltpu.get_barrier_semaphore()
     for peer in (
@@ -649,7 +659,7 @@
             ysend.at[part_rows(r)],
             xq.at[0, quarter, part_rows(r)],
             tok_s.at[0, 0],
-            tok_r.at[0, quarter, r],
+            tok_r.at[0, r],
             {"groups": 1 - g},
         )
 
@@ -658,7 +668,7 @@
             ysend2.at[part_rows(r)],
             xq.at[0, q_x, part_rows(r)],
             tok_s.at[0, 2],
-            tok_r.at[0, q_x, r],
+            tok_x.at[0, r],
             {"groups": 1 - g},
         )
 
@@ -668,33 +678,35 @@
             src,
             xq.at[k, quarter, part_rows(r)],
             tok_s.at[k, 0],
-            tok_r.at[k, quarter, r],
+            tok_r.at[k, r],
             {"seq": in_z},
         )
 
     def spread_tok(k, c, r, kind):
         slot = xq.at[k, c, part_rows(r)]
         to = {"fsdp": 1 - f} if kind == 2 else {"sub": 1 - s}
-        return remote(slot, slot, tok_s.at[k, kind], tok_r.at[k, c, r], to)
-
-    def tok_arrive(k, c, r):
-        slot = xq.at[k, c, part_rows(r)]
-        remote(slot, slot, tok_s.at[k, 1], tok_r.at[k, c, r], {"sub": 1 - s}).wait_recv()
+        sem = tok_x.at[k, r] if kind == 2 else tok_w.at[k, kind // 2]
+        return remote(slot, slot, tok_s.at[k, kind], sem, to)
+
+    def tok_arrive(k, r):
+        slot = xq.at[k, quarter, part_rows(r)]
+        remote(slot, slot, tok_s.at[k, 1], tok_r.at[k, r], {"sub": 1 - s}).wait_recv()
 
     def gather_own(k, r):
-        tok_arrive(k, quarter, r)
+        tok_arrive(k, r)
         if k > 0 or r < direct:
             spread_tok(k, quarter, r, 2).start()
         spread_tok(k, quarter, r, 1).start()
 
     def gather_fwd(k, r):
-        tok_arrive(k, q_x, r)
+        slot = xq.at[k, q_x, part_rows(r)]
+        remote(slot, slot, tok_s.at[k, 1], tok_x.at[k, r], {"sub": 1 - s}).wait_recv()
         spread_tok(k, q_x, r, 3).start()
 
-    def gathered(k, which):
-        for r in range(row_chunks):
-            for c in which:
-                tok_arrive(k, c, r)
+    def gathered(k):
+        for i, c in enumerate((q_sib, q_diag)):
+            slot = xq.at[k, c]
+            remote(slot, slot, tok_s.at[k, 1], tok_w.at[k, i], {"sub": 1 - s}).wait_recv()
 
     def both(stack):
         return pl.ds(2 * stack, 2)
@@ -1012,14 +1024,14 @@
         o_relay(second, (4, 5), False)
         gather_fwd(1, 3)
         gather_own(2, 2)
-        gathered(0, (q_sib, q_diag))
+        gathered(0)
         project(0, 0, 0, w_pieces, True)
         pl.semaphore_wait(beyond, 1)
         send_part(0, 0)
         o_relay(second, (6, 7), False)
         gather_fwd(2, 0)
         gather_own(2, 3)
-        gathered(1, (q_sib, q_diag))
+        gathered(1)
         project(1, 0, 0, w_pieces, True)
         send_qk(1, 0)
         o_relay(sl_far, range(early), False)
@@ -1030,7 +1042,7 @@
         w_relay(2)
         w_relay(3)
         gather_fwd(2, 3)
-        gathered(2, (q_sib, q_diag))
+        gathered(2)
         project(2, 0, 0, w_pieces, True)
         send_part(2, 0)
         w_relay(4)
@@ -1098,7 +1110,7 @@
     @pl.when(outer)
     def _():
         for r in range(row_chunks):
-            tok_arrive(0, quarter, r)
+            tok_arrive(0, r)
             z_tok(2, r).start()
         for c in range(w_pieces):
             w_loaded(c)
@@ -1242,7 +1254,9 @@
             dma((n,)),
             dma((n, w_pieces)),
             dma((3, 4)),
-            dma((3, pieces, row_chunks)),
+            dma((3, row_chunks)),
+            dma((3, row_chunks)),
+            dma((3, 2)),
             dma((n,)),
             dma((n,)),
             dma((n, out_pieces)),

time: 77.6 us -> 77.4 us (level)
  no operation moved by 1% of the time
where the time goes in v4:
time: 77.4 us; the launch traced here: 77.2 us
  Pallas kernels  74.9 us (97%)
  local copies, waits for them, and re-layouts  2.3 us (3%)
    pallas_call x1, Pallas kernels, per_device_line(): pl.pallas_call(functools.partial(line_kernel, n, pieces, w_pieces, out_pi...  74.9 us
    unnamed x1, local copies, waits for them, and re-layouts  2.3 us

profile of v4, /device:TPU:0, one launch (start us, length us, event | category | flops | bytes accessed | tf_op | source)
XLA Modules:
  0.0 77.2 jit_solution(12808866509066027188)
XLA Ops:
  0.0 74.9 %shard_map.73 = bf16[256,2048]{1,0:T(8,128)(2,1)} custom-call(bf16[256,8192]{1,0:T(8,128)(2,1)} %tok_hbm.1, f32[1,8192]{1,0:T(1,128)} %bitcast.10, f32[1,128]{1,0:T(1,128)} %bitcast.11, bf16[2,8,16,2048]{3,2,1,0:T(8,128)(2,1)} %bitcast.6, bf16[8,8192]{1,0:T(8,128)(2,1)} %bitcast.8, bf16[8,8192]{1,0:T(8,128)(2,1)} %bitcast.9, bf16[64,8192]{1,0:T(8,128)(2,1)} %bitcast.7), custom_call_target="tpu_custom_call" | custom-call | tf_op jit(solution)/shard_map/pallas_call | solution.py:1222
  74.9 2.3 %copy.9 = bf16[256,2048]{1,0:T(8,128)(2,1)} copy(bf16[256,2048]{1,0:T(8,128)(2,1)} %shard_map.73) | data formatting | bytes 2097152
